TPU v7x, 32 devices: a whole 2x2x4 slice. The times are simulated.
32 devices in a mesh: ccy: 4 (over x, core), path: 8 (over z, y).
Axes of the slice: x: 2, y: 2, z: 4, core: 2. Of those that a mesh axis runs over, the one named last changes fastest.
Arguments:
- curve_store: bfloat16 [4, 16, 64, 2048], P('ccy', 'path'), may hold values from -0.13 to 0.18
- cash_index: int32 [4, 2048, 16], P('ccy'), may hold values from 0 to 1023
- cash_amount: float32 [4, 2048, 16], P('ccy'), may hold values from -0.6 to 0.6
- trade_set: int32 [4, 2048], P('ccy'), may hold values from 0 to 511
- date_slot: int32 [16], replicated, may hold values from 0 to 15, as said below
- default_weight: float32 [16, 512], replicated, may hold values from 0.02 to 0.2
Outputs:
- exposure: float32 [16, 512], P(None, 'ccy')
- node_sens: float32 [4, 16, 64], P('ccy')
Inputs may be any that keep to these rules, and one draw needn't show every extreme that they name: `date_slot`: the 16 slots are distinct; slot s is stored at path index s // 2, position s % 2.
All inputs are finite; a program needn't handle non-finite values.
Results may differ from a plain program's by a relative error of at most 0.0029.
Values may be sent and summed in bfloat16 or wider, within the bound.
No kernel may reach another device: no remote copies, remote signals or barrier semaphores. Data moves between devices by JAX's collectives and lax.ppermute only.
A program may use at most 64 MiB of HBM per device.

v0:
```python
import jax
import jax.numpy as jnp
from jax import lax
from jax.sharding import PartitionSpec as P

NODES = 64
CFG = 1024
NSETS = 512
DATES = 16
PATHS_DEV = 256


SOFTEN = 0.04
HORIZON = 32.0


def date_tables(date_index, node_count, grid_count):
    start_time = 0.5 * (jnp.asarray(date_index).astype(jnp.float32) + 1.0)
    grid_times = HORIZON * (jnp.arange(grid_count, dtype=jnp.float32) + 1.0) / grid_count
    tenors = HORIZON * (jnp.arange(node_count, dtype=jnp.float32) + 1.0) / node_count
    remain = grid_times - start_time
    alive_mask = (remain > 0.0).astype(jnp.float32)
    clipped = jnp.clip(remain, HORIZON / node_count, HORIZON)
    weights = jnp.maximum(
        0.0, 1.0 - jnp.abs(clipped[None, :] - tenors[:, None]) * (node_count / HORIZON)
    )
    return (remain, alive_mask, weights)


def netted_cash(flow_index, amount, trade_sets):
    columns = jnp.repeat(trade_sets, flow_index.shape[1])
    cash_table = (
        jnp.zeros((CFG, NSETS), jnp.float32)
        .at[flow_index.reshape(-1), columns]
        .add(amount.reshape(-1))
    )
    return cash_table.astype(jnp.bfloat16)


def local(curve_store, cash_index, cash_amount, trade_set, date_slot, default_weight):
    groups = lax.axis_size("ccy")
    group_index = lax.axis_index("ccy")
    share_size = NSETS // groups
    total_paths = PATHS_DEV * lax.axis_size("path")
    cash_table = netted_cash(cash_index[0], cash_amount[0], trade_set[0])
    blocks = lax.all_to_all(curve_store, "path", split_axis=3, concat_axis=1, tiled=True)[0]
    cash_all = lax.all_gather(cash_table[None], "ccy", axis=0, tiled=True)

    def fetch_curve(slot_id):
        found = lax.dynamic_index_in_dim(blocks, slot_id, 0, keepdims=False)
        return found

    def advance(unused, inputs):
        date_index, slot_id, weight_row = inputs
        remain, alive_mask, weights = date_tables(date_index, NODES, CFG)
        grid_weights = weights.astype(jnp.bfloat16)
        curve_now = fetch_curve(slot_id)
        curve_groups = lax.all_gather(curve_now[None], "ccy", axis=0, tiled=True)
        yields = jnp.einsum(
            "gnp,nc->gpc", curve_groups, grid_weights, preferred_element_type=jnp.float32
        )
        discount_all = alive_mask * jnp.exp(-yields * remain)
        values = jnp.einsum(
            "gpc,gcs->ps",
            discount_all.astype(jnp.bfloat16),
            cash_all,
            preferred_element_type=jnp.float32,
        )
        discount = lax.dynamic_index_in_dim(discount_all, group_index, 0, keepdims=False)
        rooted = jnp.sqrt(values * values + SOFTEN)
        slopes = (weight_row / total_paths * 0.5 * (1.0 + values / rooted)).astype(jnp.bfloat16)
        share_values = lax.dynamic_slice_in_dim(values, group_index * share_size, share_size, 1)
        share_root = lax.dynamic_slice_in_dim(rooted, group_index * share_size, share_size, 1)
        exposure_part = jnp.sum(0.5 * (share_values + share_root), axis=0) / total_paths
        back_flow = lax.dot_general(
            slopes, cash_table, (((1,), (1,)), ((), ())), preferred_element_type=jnp.float32
        )
        node_pull = jnp.sum(back_flow * -remain * discount, axis=0)
        sens_part = jnp.dot(weights, node_pull, precision=lax.Precision.HIGHEST)
        exposure_part, sens_part = lax.psum((exposure_part, sens_part), "path")
        return (unused, (exposure_part, sens_part))

    inputs = (jnp.arange(DATES, dtype=jnp.int32), date_slot, default_weight)
    unused, (exposure_rows, sens_rows) = lax.scan(advance, jnp.zeros((), jnp.float32), inputs)
    return (exposure_rows, sens_rows[None])


def solution(mesh):
    in_specs = (
        P("ccy", "path", None, None),
        P("ccy", None, None),
        P("ccy", None, None),
        P("ccy", None),
        P(),
        P(),
    )
    out_specs = (P(None, "ccy"), P("ccy", None, None))
    return jax.shard_map(local, mesh=mesh, in_specs=in_specs, out_specs=out_specs, check_vma=False)
```

profile of v0, /device:TPU:0, one launch (start us, length us, event | category | flops | bytes accessed | tf_op | source)
XLA Modules:
  0.0 758.6 jit_solution(14273269540718407822)
XLA Ops:
  12.4 171.6 %scatter_custom_fusion = f32[524288]{0:T(1024)S(1)} fusion(s32[32768]{0:T(1024)S(1)} %broadcast_select_fusion, f32[32768]{0:T(1024)S(1)} %reshape.107, f32[]{:T(128)} %constant.137.clone.1), kind=kCustom, calls=%fused_computation.43 | custom fusion | flops 32768 | bytes 2097156
  184.1 1.5 broadcast_in_dim.47
  185.6 2.4 copy.12
  188.0 1.5 reshape.117
  189.5 7.3 all-to-all-start
  197.5 13.8 %all-to-all-done = bf16[8,2,16384]{2,1,0:T(2,128)(2,1)S(1)} async-done(((bf16[8,2,16384]{2,1,0:T(2,128)(2,1)}), bf16[8,2,16384]{2,1,0:T(2,128)(2,1)S(1)}, u32[]{:S(2)}, u32[]{:S(2)}) %all-to-all-start) | async-done | bytes 524320 | tf_op jit(solution)/shard_map/all_to_all | solution.py:46
  212.6 10.3 %all-gather.2.cloned.1.call-done = bf16[4,1024,512]{2,1,0:T(8,128)(2,1)} async-done(((bf16[1,1024,512]{2,1,0:T(8,128)(2,1)}), bf16[4,1024,512]{2,1,0:T(8,128)(2,1)}) %all-gather.2.cloned.1.call-update) | async-done | bytes 4194320 | tf_op jit(solution)/shard_map/all_gather | solution.py:47
  222.9 528.2 %while.15 = (s32[]{:T(128)}, f32[16,128]{1,0:T(8,128)S(1)}, f32[16,64]{1,0:T(8,128)}, s32[16]{0:T(128)S(1)}, s32[16]{0:T(128)S(1)}, /*index=5*/bf16[16,64,256]{2...) while((s32[]{:T(128)}, f32[16,128]{1,0:T(8,128)S(1)}, ...), condition=%wide.region_6.7_spmd, body=%wide.region_1.6_spmd.sunk | while | flops 1484043008 | bytes 33709876 | solution.py:84
  225.4 5.5 all_gather.12
  233.2 1.3 add_sqrt_fusion.3
  236.3 21.4 %all-reduce.2 = (f32[1,128]{1,0:T(1,128)S(1)}, f32[1,64]{1,0:T(1,128)S(1)}) all-reduce(f32[1,128]{1,0:T(1,128)S(1)} %multiply_bitcast_fusion.2, f32[1,64]{1,0:T(1,128)S(1)} %fusion.54), channel_id=1, replica_groups=mesh['ccy'=4,'path'=8] {'path'}, use_global_device_ids=true, to_apply=%region_3.3 | all-reduce | flops 192 | bytes 1536 | tf_op jit(solution)/shard_map/while/body/eval_jaxpr/psum | solution.py:80
  257.8 1.3 dynamic_update_slice.19
  261.5 5.5 all_gather.12
  269.3 1.3 add_sqrt_fusion.3
  272.4 17.2 %all-reduce.2 = (f32[1,128]{1,0:T(1,128)S(1)}, f32[1,64]{1,0:T(1,128)S(1)}) all-reduce(f32[1,128]{1,0:T(1,128)S(1)} %multiply_bitcast_fusion.2, f32[1,64]{1,0:T(1,128)S(1)} %fusion.54), channel_id=1, replica_groups=mesh['ccy'=4,'path'=8] {'path'}, use_global_device_ids=true, to_apply=%region_3.3 | all-reduce | flops 192 | bytes 1536 | tf_op jit(solution)/shard_map/while/body/eval_jaxpr/psum | solution.py:80
  289.6 1.3 dynamic_update_slice.19
  293.4 5.5 all_gather.12
  301.2 1.3 add_sqrt_fusion.3
  304.3 19.2 %all-reduce.2 = (f32[1,128]{1,0:T(1,128)S(1)}, f32[1,64]{1,0:T(1,128)S(1)}) all-reduce(f32[1,128]{1,0:T(1,128)S(1)} %multiply_bitcast_fusion.2, f32[1,64]{1,0:T(1,128)S(1)} %fusion.54), channel_id=1, replica_groups=mesh['ccy'=4,'path'=8] {'path'}, use_global_device_ids=true, to_apply=%region_3.3 | all-reduce | flops 192 | bytes 1536 | tf_op jit(solution)/shard_map/while/body/eval_jaxpr/psum | solution.py:80
  327.3 5.5 all_gather.12
  335.1 1.3 add_sqrt_fusion.3
  338.2 17.2 %all-reduce.2 = (f32[1,128]{1,0:T(1,128)S(1)}, f32[1,64]{1,0:T(1,128)S(1)}) all-reduce(f32[1,128]{1,0:T(1,128)S(1)} %multiply_bitcast_fusion.2, f32[1,64]{1,0:T(1,128)S(1)} %fusion.54), channel_id=1, replica_groups=mesh['ccy'=4,'path'=8] {'path'}, use_global_device_ids=true, to_apply=%region_3.3 | all-reduce | flops 192 | bytes 1536 | tf_op jit(solution)/shard_map/while/body/eval_jaxpr/psum | solution.py:80
  359.1 5.5 all_gather.12
  366.9 1.3 add_sqrt_fusion.3
  370.1 19.2 %all-reduce.2 = (f32[1,128]{1,0:T(1,128)S(1)}, f32[1,64]{1,0:T(1,128)S(1)}) all-reduce(f32[1,128]{1,0:T(1,128)S(1)} %multiply_bitcast_fusion.2, f32[1,64]{1,0:T(1,128)S(1)} %fusion.54), channel_id=1, replica_groups=mesh['ccy'=4,'path'=8] {'path'}, use_global_device_ids=true, to_apply=%region_3.3 | all-reduce | flops 192 | bytes 1536 | tf_op jit(solution)/shard_map/while/body/eval_jaxpr/psum | solution.py:80
  389.3 1.3 dynamic_update_slice.19
  393.0 5.5 all_gather.12
  400.8 1.3 add_sqrt_fusion.3
  403.9 17.2 %all-reduce.2 = (f32[1,128]{1,0:T(1,128)S(1)}, f32[1,64]{1,0:T(1,128)S(1)}) all-reduce(f32[1,128]{1,0:T(1,128)S(1)} %multiply_bitcast_fusion.2, f32[1,64]{1,0:T(1,128)S(1)} %fusion.54), channel_id=1, replica_groups=mesh['ccy'=4,'path'=8] {'path'}, use_global_device_ids=true, to_apply=%region_3.3 | all-reduce | flops 192 | bytes 1536 | tf_op jit(solution)/shard_map/while/body/eval_jaxpr/psum | solution.py:80
  424.9 5.5 all_gather.12
  432.7 1.3 add_sqrt_fusion.3
  435.8 19.2 %all-reduce.2 = (f32[1,128]{1,0:T(1,128)S(1)}, f32[1,64]{1,0:T(1,128)S(1)}) all-reduce(f32[1,128]{1,0:T(1,128)S(1)} %multiply_bitcast_fusion.2, f32[1,64]{1,0:T(1,128)S(1)} %fusion.54), channel_id=1, replica_groups=mesh['ccy'=4,'path'=8] {'path'}, use_global_device_ids=true, to_apply=%region_3.3 | all-reduce | flops 192 | bytes 1536 | tf_op jit(solution)/shard_map/while/body/eval_jaxpr/psum | solution.py:80
  455.0 1.3 dynamic_update_slice.19
  458.8 5.5 all_gather.12
  466.6 1.3 add_sqrt_fusion.3
  469.7 17.2 %all-reduce.2 = (f32[1,128]{1,0:T(1,128)S(1)}, f32[1,64]{1,0:T(1,128)S(1)}) all-reduce(f32[1,128]{1,0:T(1,128)S(1)} %multiply_bitcast_fusion.2, f32[1,64]{1,0:T(1,128)S(1)} %fusion.54), channel_id=1, replica_groups=mesh['ccy'=4,'path'=8] {'path'}, use_global_device_ids=true, to_apply=%region_3.3 | all-reduce | flops 192 | bytes 1536 | tf_op jit(solution)/shard_map/while/body/eval_jaxpr/psum | solution.py:80
  490.6 5.5 all_gather.12
  498.4 1.3 add_sqrt_fusion.3
  501.6 19.2 %all-reduce.2 = (f32[1,128]{1,0:T(1,128)S(1)}, f32[1,64]{1,0:T(1,128)S(1)}) all-reduce(f32[1,128]{1,0:T(1,128)S(1)} %multiply_bitcast_fusion.2, f32[1,64]{1,0:T(1,128)S(1)} %fusion.54), channel_id=1, replica_groups=mesh['ccy'=4,'path'=8] {'path'}, use_global_device_ids=true, to_apply=%region_3.3 | all-reduce | flops 192 | bytes 1536 | tf_op jit(solution)/shard_map/while/body/eval_jaxpr/psum | solution.py:80
  520.8 1.3 dynamic_update_slice.19
  524.5 5.5 all_gather.12
  532.3 1.3 add_sqrt_fusion.3
  535.4 17.2 %all-reduce.2 = (f32[1,128]{1,0:T(1,128)S(1)}, f32[1,64]{1,0:T(1,128)S(1)}) all-reduce(f32[1,128]{1,0:T(1,128)S(1)} %multiply_bitcast_fusion.2, f32[1,64]{1,0:T(1,128)S(1)} %fusion.54), channel_id=1, replica_groups=mesh['ccy'=4,'path'=8] {'path'}, use_global_device_ids=true, to_apply=%region_3.3 | all-reduce | flops 192 | bytes 1536 | tf_op jit(solution)/shard_map/while/body/eval_jaxpr/psum | solution.py:80
  556.4 5.5 all_gather.12
  564.2 1.3 add_sqrt_fusion.3
  567.3 19.2 %all-reduce.2 = (f32[1,128]{1,0:T(1,128)S(1)}, f32[1,64]{1,0:T(1,128)S(1)}) all-reduce(f32[1,128]{1,0:T(1,128)S(1)} %multiply_bitcast_fusion.2, f32[1,64]{1,0:T(1,128)S(1)} %fusion.54), channel_id=1, replica_groups=mesh['ccy'=4,'path'=8] {'path'}, use_global_device_ids=true, to_apply=%region_3.3 | all-reduce | flops 192 | bytes 1536 | tf_op jit(solution)/shard_map/while/body/eval_jaxpr/psum | solution.py:80
  586.5 1.3 dynamic_update_slice.19
  590.3 5.5 all_gather.12
  598.1 1.3 add_sqrt_fusion.3
  601.2 17.2 %all-reduce.2 = (f32[1,128]{1,0:T(1,128)S(1)}, f32[1,64]{1,0:T(1,128)S(1)}) all-reduce(f32[1,128]{1,0:T(1,128)S(1)} %multiply_bitcast_fusion.2, f32[1,64]{1,0:T(1,128)S(1)} %fusion.54), channel_id=1, replica_groups=mesh['ccy'=4,'path'=8] {'path'}, use_global_device_ids=true, to_apply=%region_3.3 | all-reduce | flops 192 | bytes 1536 | tf_op jit(solution)/shard_map/while/body/eval_jaxpr/psum | solution.py:80
  622.2 5.5 all_gather.12
  629.9 1.3 add_sqrt_fusion.3
  633.1 19.2 %all-reduce.2 = (f32[1,128]{1,0:T(1,128)S(1)}, f32[1,64]{1,0:T(1,128)S(1)}) all-reduce(f32[1,128]{1,0:T(1,128)S(1)} %multiply_bitcast_fusion.2, f32[1,64]{1,0:T(1,128)S(1)} %fusion.54), channel_id=1, replica_groups=mesh['ccy'=4,'path'=8] {'path'}, use_global_device_ids=true, to_apply=%region_3.3 | all-reduce | flops 192 | bytes 1536 | tf_op jit(solution)/shard_map/while/body/eval_jaxpr/psum | solution.py:80
  656.0 5.5 all_gather.12
  663.8 1.3 add_sqrt_fusion.3
  666.9 17.2 %all-reduce.2 = (f32[1,128]{1,0:T(1,128)S(1)}, f32[1,64]{1,0:T(1,128)S(1)}) all-reduce(f32[1,128]{1,0:T(1,128)S(1)} %multiply_bitcast_fusion.2, f32[1,64]{1,0:T(1,128)S(1)} %fusion.54), channel_id=1, replica_groups=mesh['ccy'=4,'path'=8] {'path'}, use_global_device_ids=true, to_apply=%region_3.3 | all-reduce | flops 192 | bytes 1536 | tf_op jit(solution)/shard_map/while/body/eval_jaxpr/psum | solution.py:80
  684.1 1.3 dynamic_update_slice.19
  687.9 5.5 all_gather.12
  695.7 1.3 add_sqrt_fusion.3
  698.8 19.2 %all-reduce.2 = (f32[1,128]{1,0:T(1,128)S(1)}, f32[1,64]{1,0:T(1,128)S(1)}) all-reduce(f32[1,128]{1,0:T(1,128)S(1)} %multiply_bitcast_fusion.2, f32[1,64]{1,0:T(1,128)S(1)} %fusion.54), channel_id=1, replica_groups=mesh['ccy'=4,'path'=8] {'path'}, use_global_device_ids=true, to_apply=%region_3.3 | all-reduce | flops 192 | bytes 1536 | tf_op jit(solution)/shard_map/while/body/eval_jaxpr/psum | solution.py:80
  721.8 5.5 all_gather.12
  729.6 1.3 add_sqrt_fusion.3
  732.7 17.2 %all-reduce.2 = (f32[1,128]{1,0:T(1,128)S(1)}, f32[1,64]{1,0:T(1,128)S(1)}) all-reduce(f32[1,128]{1,0:T(1,128)S(1)} %multiply_bitcast_fusion.2, f32[1,64]{1,0:T(1,128)S(1)} %fusion.54), channel_id=1, replica_groups=mesh['ccy'=4,'path'=8] {'path'}, use_global_device_ids=true, to_apply=%region_3.3 | all-reduce | flops 192 | bytes 1536 | tf_op jit(solution)/shard_map/while/body/eval_jaxpr/psum | solution.py:80
  749.9 1.3 dynamic_update_slice.19
  (293 shorter events, 81.7 us)
Async XLA Ops:
  7.2 3.5 copy-start.2
  7.2 4.1 copy-start.3
  7.2 4.6 copy-start.1
  7.2 215.7 %all-gather.2.cloned.1.call-start = ((), (), s32[]{:S(2)}) async-start(), calls=%async_computation.1 | async-start | bytes 5242880 | tf_op jit(solution)/shard_map/all_gather | solution.py:47
  188.0 35.0 %copy-start.5 = (s32[16]{0:T(128)S(1)}, s32[16]{0:T(128)}, u32[]{:S(2)}) copy-start(s32[16]{0:T(128)} %param.12) | copy-start | bytes 196
  189.5 21.8 %all-to-all-start = ((bf16[8,2,16384]{2,1,0:T(2,128)(2,1)}), bf16[8,2,16384]{2,1,0:T(2,128)(2,1)S(1)}, u32[]{:S(2)}, u32[]{:S(2)}) async-start(bf16[8,2,16384]{2,1,0:T(2,128)(2,1)} %reshape.117), calls=%async_computation | async-start | bytes 1048576 | tf_op jit(solution)/shard_map/all_to_all | solution.py:46
  225.4 7.8 %copy-start = (bf16[4,1024,512]{2,1,0:T(8,128)(2,1)S(1)}, bf16[4,1024,512]{2,1,0:T(8,128)(2,1)}, u32[]{:S(2)}) copy-start(bf16[4,1024,512]{2,1,0:T(8,128)(2,1)} %get-tuple-element.337) | copy-start | bytes 12582916 | tf_op jit(solution)/shard_map/while
  261.5 7.8 %copy-start = (bf16[4,1024,512]{2,1,0:T(8,128)(2,1)S(1)}, bf16[4,1024,512]{2,1,0:T(8,128)(2,1)}, u32[]{:S(2)}) copy-start(bf16[4,1024,512]{2,1,0:T(8,128)(2,1)} %get-tuple-element.337) | copy-start | bytes 12582916 | tf_op jit(solution)/shard_map/while
  293.4 7.8 %copy-start = (bf16[4,1024,512]{2,1,0:T(8,128)(2,1)S(1)}, bf16[4,1024,512]{2,1,0:T(8,128)(2,1)}, u32[]{:S(2)}) copy-start(bf16[4,1024,512]{2,1,0:T(8,128)(2,1)} %get-tuple-element.337) | copy-start | bytes 12582916 | tf_op jit(solution)/shard_map/while
  327.2 7.8 %copy-start = (bf16[4,1024,512]{2,1,0:T(8,128)(2,1)S(1)}, bf16[4,1024,512]{2,1,0:T(8,128)(2,1)}, u32[]{:S(2)}) copy-start(bf16[4,1024,512]{2,1,0:T(8,128)(2,1)} %get-tuple-element.337) | copy-start | bytes 12582916 | tf_op jit(solution)/shard_map/while
  359.1 7.8 %copy-start = (bf16[4,1024,512]{2,1,0:T(8,128)(2,1)S(1)}, bf16[4,1024,512]{2,1,0:T(8,128)(2,1)}, u32[]{:S(2)}) copy-start(bf16[4,1024,512]{2,1,0:T(8,128)(2,1)} %get-tuple-element.337) | copy-start | bytes 12582916 | tf_op jit(solution)/shard_map/while
  393.0 7.8 %copy-start = (bf16[4,1024,512]{2,1,0:T(8,128)(2,1)S(1)}, bf16[4,1024,512]{2,1,0:T(8,128)(2,1)}, u32[]{:S(2)}) copy-start(bf16[4,1024,512]{2,1,0:T(8,128)(2,1)} %get-tuple-element.337) | copy-start | bytes 12582916 | tf_op jit(solution)/shard_map/while
  424.9 7.8 %copy-start = (bf16[4,1024,512]{2,1,0:T(8,128)(2,1)S(1)}, bf16[4,1024,512]{2,1,0:T(8,128)(2,1)}, u32[]{:S(2)}) copy-start(bf16[4,1024,512]{2,1,0:T(8,128)(2,1)} %get-tuple-element.337) | copy-start | bytes 12582916 | tf_op jit(solution)/shard_map/while
  458.7 7.8 %copy-start = (bf16[4,1024,512]{2,1,0:T(8,128)(2,1)S(1)}, bf16[4,1024,512]{2,1,0:T(8,128)(2,1)}, u32[]{:S(2)}) copy-start(bf16[4,1024,512]{2,1,0:T(8,128)(2,1)} %get-tuple-element.337) | copy-start | bytes 12582916 | tf_op jit(solution)/shard_map/while
  490.6 7.8 %copy-start = (bf16[4,1024,512]{2,1,0:T(8,128)(2,1)S(1)}, bf16[4,1024,512]{2,1,0:T(8,128)(2,1)}, u32[]{:S(2)}) copy-start(bf16[4,1024,512]{2,1,0:T(8,128)(2,1)} %get-tuple-element.337) | copy-start | bytes 12582916 | tf_op jit(solution)/shard_map/while
  524.5 7.8 %copy-start = (bf16[4,1024,512]{2,1,0:T(8,128)(2,1)S(1)}, bf16[4,1024,512]{2,1,0:T(8,128)(2,1)}, u32[]{:S(2)}) copy-start(bf16[4,1024,512]{2,1,0:T(8,128)(2,1)} %get-tuple-element.337) | copy-start | bytes 12582916 | tf_op jit(solution)/shard_map/while
  556.4 7.8 %copy-start = (bf16[4,1024,512]{2,1,0:T(8,128)(2,1)S(1)}, bf16[4,1024,512]{2,1,0:T(8,128)(2,1)}, u32[]{:S(2)}) copy-start(bf16[4,1024,512]{2,1,0:T(8,128)(2,1)} %get-tuple-element.337) | copy-start | bytes 12582916 | tf_op jit(solution)/shard_map/while
  590.3 7.8 %copy-start = (bf16[4,1024,512]{2,1,0:T(8,128)(2,1)S(1)}, bf16[4,1024,512]{2,1,0:T(8,128)(2,1)}, u32[]{:S(2)}) copy-start(bf16[4,1024,512]{2,1,0:T(8,128)(2,1)} %get-tuple-element.337) | copy-start | bytes 12582916 | tf_op jit(solution)/shard_map/while
  622.1 7.8 %copy-start = (bf16[4,1024,512]{2,1,0:T(8,128)(2,1)S(1)}, bf16[4,1024,512]{2,1,0:T(8,128)(2,1)}, u32[]{:S(2)}) copy-start(bf16[4,1024,512]{2,1,0:T(8,128)(2,1)} %get-tuple-element.337) | copy-start | bytes 12582916 | tf_op jit(solution)/shard_map/while
  656.0 7.8 %copy-start = (bf16[4,1024,512]{2,1,0:T(8,128)(2,1)S(1)}, bf16[4,1024,512]{2,1,0:T(8,128)(2,1)}, u32[]{:S(2)}) copy-start(bf16[4,1024,512]{2,1,0:T(8,128)(2,1)} %get-tuple-element.337) | copy-start | bytes 12582916 | tf_op jit(solution)/shard_map/while
  687.9 7.8 %copy-start = (bf16[4,1024,512]{2,1,0:T(8,128)(2,1)S(1)}, bf16[4,1024,512]{2,1,0:T(8,128)(2,1)}, u32[]{:S(2)}) copy-start(bf16[4,1024,512]{2,1,0:T(8,128)(2,1)} %get-tuple-element.337) | copy-start | bytes 12582916 | tf_op jit(solution)/shard_map/while
  721.8 7.8 %copy-start = (bf16[4,1024,512]{2,1,0:T(8,128)(2,1)S(1)}, bf16[4,1024,512]{2,1,0:T(8,128)(2,1)}, u32[]{:S(2)}) copy-start(bf16[4,1024,512]{2,1,0:T(8,128)(2,1)} %get-tuple-element.337) | copy-start | bytes 12582916 | tf_op jit(solution)/shard_map/while
  751.2 0.6 copy-start.4
Sparse Core Ops, SparseCore 0:
  185.7 37.1 all-gather.1
where the time goes:
time: 762 us; the launch traced here: 759 us
  blocking collectives  382 us (50%)
  other arithmetic  187 us (25%)
  matrix products  52 us (7%)
  local copies, waits for them, and re-layouts  51.8 us (7%)
  loops' own time  40.8 us (5%)
  waiting for transfers between devices  24.2 us (3%)
  between operations  14.2 us (2%)
    psum x16, blocking collectives, advance(): exposure_part, sens_part = lax.psum((exposure_part, sens_part), 'path')  293 us
    unnamed x4, other arithmetic  173 us
    all_gather x16, blocking collectives, advance(): curve_groups = lax.all_gather(curve_now[None], 'ccy', axis=0, tiled=True)  88.8 us
    another operation x1, loops' own time, local(): lax.scan(advance, jnp.zeros((), jnp.float32), inputs)  40.8 us
    dot_general x16, matrix products, advance(): jnp.einsum('gpc,gcs->ps', discount_all.astype(jnp.bfloat16), cash_all, pr...  21.4 us
    dynamic_update_slice x32, local copies, waits for them, and re-layouts, local(): lax.scan(advance, jnp.zeros((), jnp.float32), inputs)  21.1 us
    dynamic_slice x32, local copies, waits for them, and re-layouts, local(): lax.scan(advance, jnp.zeros((), jnp.float32), inputs)  18.9 us
  transfers between devices with their start and end apart: 2, of which 2 were waited for; matrix products, arithmetic and copies ran while one was open for 1% of the time, Pallas kernels for 0%

commit v1 on v0

v1 whole, which is shorter than its diff:
```python
import functools
import math

import jax
import jax.numpy as jnp
from jax import lax
from jax.experimental import pallas as pl
from jax.experimental.pallas import tpu as pltpu
from jax.sharding import PartitionSpec as P

CFG = 1024
NSETS = 512
SOFTEN = 0.04
HORIZON = 32.0
LOG2E = math.log2(math.e)
VMEM_LIMIT = 56 * 1024 * 1024

NT = (((1,), (1,)), ((), ()))
NN = (((1,), (0,)), ((), ()))


def dot32(a, b, dims):
    return lax.dot_general(a, b, dims, preferred_element_type=jnp.float32)


def table_kernel(idx_ref, amt_ref, set_ref, out_ref, idx_t, hi_t, lo_t, flow_ref, set_oh):
    ncf, trades = idx_ref.shape
    nsets, cfg = out_ref.shape
    sub, lanes, rows = 16, 128, 64
    idx = idx_ref[...]
    total = jnp.zeros((ncf, trades), jnp.float32)
    for k in range(ncf):
        same = idx == idx_ref[k : k + 1, :]
        total = total + jnp.where(same, amt_ref[k : k + 1, :], 0.0)
    high = total.astype(jnp.bfloat16).astype(jnp.float32)
    low = total - high
    for k in range(ncf):
        row = slice(k * sub, (k + 1) * sub)
        shape = (sub, trades)
        idx_t[row, :] = jnp.broadcast_to(idx[k : k + 1, :], shape).astype(jnp.int16)
        hi_t[row, :] = jnp.broadcast_to(high[k : k + 1, :], shape).astype(jnp.bfloat16)
        lo_t[row, :] = jnp.broadcast_to(low[k : k + 1, :], shape).astype(jnp.bfloat16)
    set_rows = lax.broadcasted_iota(jnp.int32, (nsets, trades), 0)
    one_hot = jnp.where(set_rows == set_ref[...], 1.0, 0.0).astype(jnp.bfloat16)
    set_oh[:, :trades] = one_hot
    set_oh[:, trades:] = one_hot

    tiles = rows // sub
    base = lax.broadcasted_iota(jnp.int32, (tiles, sub, lanes), 0) * sub
    base = base + lax.broadcasted_iota(jnp.int32, (tiles, sub, lanes), 1)

    def fill(step, carry):
        block = step // (cfg // rows)
        c0 = (step % (cfg // rows)) * rows
        cols = pl.ds(pl.multiple_of(block * lanes, lanes), lanes)
        lcols = pl.ds(pl.multiple_of(trades + block * lanes, lanes), lanes)
        dates = (base + c0).astype(jnp.int16)
        acc_hi = jnp.zeros((tiles, sub, lanes), jnp.bfloat16)
        acc_lo = jnp.zeros((tiles, sub, lanes), jnp.bfloat16)
        for k in range(ncf):
            row = slice(k * sub, (k + 1) * sub)
            hit = dates == idx_t[row, cols][None]
            acc_hi = jnp.where(hit, hi_t[row, cols][None], acc_hi)
            acc_lo = jnp.where(hit, lo_t[row, cols][None], acc_lo)
        out_rows = pl.ds(pl.multiple_of(c0, rows), rows)
        flow_ref[out_rows, cols] = acc_hi.reshape(rows, lanes)
        flow_ref[out_rows, lcols] = acc_lo.reshape(rows, lanes)
        return carry

    lax.fori_loop(0, (trades // lanes) * (cfg // rows), fill, 0)
    half = 256
    for c0 in range(0, cfg, half):
        block = dot32(set_oh[...], flow_ref[c0 : c0 + half, :], NT)
        out_ref[:, c0 : c0 + half] = block.astype(jnp.bfloat16)


def build_table(idx, amt, sets):
    ncf, trades = idx.shape
    return pl.pallas_call(
        table_kernel,
        out_shape=jax.ShapeDtypeStruct((NSETS, CFG), jnp.bfloat16),
        in_specs=[pl.BlockSpec(memory_space=pltpu.VMEM)] * 3,
        out_specs=pl.BlockSpec(memory_space=pltpu.VMEM),
        scratch_shapes=[
            pltpu.VMEM((ncf * 16, trades), jnp.int16),
            pltpu.VMEM((ncf * 16, trades), jnp.bfloat16),
            pltpu.VMEM((ncf * 16, trades), jnp.bfloat16),
            pltpu.VMEM((CFG, 2 * trades), jnp.bfloat16),
            pltpu.VMEM((NSETS, 2 * trades), jnp.bfloat16),
        ],
        cost_estimate=pl.CostEstimate(
            flops=4 * trades * NSETS * CFG, bytes_accessed=2**21, transcendentals=0
        ),
        compiler_params=pltpu.CompilerParams(vmem_limit_bytes=VMEM_LIMIT),
        name="table",
    )(idx, amt, sets)


def disc_kernel(date_ref, *refs):
    groups = (len(refs) - 3) // 1
    curves, (disc_ref, scaled_ref, rhs) = refs[: len(refs) - 3], refs[len(refs) - 3 :]
    slots, nodes, paths = curves[0].shape
    cfg = disc_ref.shape[2]
    depth = rhs.shape[0]
    for k in range(slots):
        date = date_ref[k]
        start = 0.5 * (date.astype(jnp.float32) + 1.0)
        grid = lax.broadcasted_iota(jnp.int32, (cfg, nodes), 0).astype(jnp.float32)
        remain = HORIZON * (grid + 1.0) / cfg - start
        node = lax.broadcasted_iota(jnp.int32, (cfg, nodes), 1).astype(jnp.float32)
        tenor = HORIZON * (node + 1.0) / nodes
        clipped = jnp.clip(remain, HORIZON / nodes, HORIZON)
        weight = jnp.maximum(0.0, 1.0 - jnp.abs(clipped - tenor) * (nodes / HORIZON))
        scaled = weight * (remain * (-LOG2E))
        scaled_ref[k] = weight * -remain
        high = scaled.astype(jnp.bfloat16)
        rest = scaled - high.astype(jnp.float32)
        mid = rest.astype(jnp.bfloat16)
        low = (rest - mid.astype(jnp.float32)).astype(jnp.bfloat16)
        column = lax.broadcasted_iota(jnp.int32, (cfg, depth - 3 * nodes), 1)
        late = lax.broadcasted_iota(jnp.int32, (cfg, depth - 3 * nodes), 0)
        late = HORIZON * (late.astype(jnp.float32) + 1.0) / cfg - start
        dead = jnp.where((column == 0) & (late <= 0.0), -1e30, 0.0).astype(jnp.bfloat16)
        lhs = jnp.concatenate([high, mid, low, dead], axis=1)
        for g in range(groups):
            part = curves[g][k]
            for copy in range(3):
                rhs[copy * nodes : (copy + 1) * nodes, :] = part
            rhs[3 * nodes :, :] = jnp.ones((depth - 3 * nodes, paths), jnp.bfloat16)
            disc_ref[k, g] = jnp.exp2(dot32(lhs, rhs[...], NN)).astype(jnp.bfloat16)


def discounts(dates, curves):
    slots, nodes, paths = curves[0].shape
    groups = len(curves)
    return pl.pallas_call(
        disc_kernel,
        out_shape=(
            jax.ShapeDtypeStruct((slots, groups, CFG, paths), jnp.bfloat16),
            jax.ShapeDtypeStruct((slots, CFG, nodes), jnp.float32),
        ),
        in_specs=[pl.BlockSpec(memory_space=pltpu.SMEM)]
        + [pl.BlockSpec(memory_space=pltpu.VMEM)] * groups,
        out_specs=(pl.BlockSpec(memory_space=pltpu.VMEM),) * 2,
        scratch_shapes=[pltpu.VMEM((4 * nodes, paths), jnp.bfloat16)],
        cost_estimate=pl.CostEstimate(
            flops=2 * slots * groups * CFG * paths * 4 * nodes,
            bytes_accessed=2 * slots * groups * CFG * paths,
            transcendentals=slots * groups * CFG * paths,
        ),
        compiler_params=pltpu.CompilerParams(vmem_limit_bytes=VMEM_LIMIT),
        name="discounts",
    )(dates, *curves)


def price_kernel(scale, weight_ref, scaled_ref, disc_ref, *refs):
    groups = disc_ref.shape[1]
    tables = refs[:groups]
    expo_ref, sens_ref, value_ref, slope_ref, pull_ref = refs[groups:]
    slots = disc_ref.shape[0]
    nsets, cfg = tables[0].shape
    paths = disc_ref.shape[3]
    lanes = 128
    for k in range(slots):
        value = dot32(tables[0][...], disc_ref[k, 0], NN)
        for g in range(1, groups):
            value = value + dot32(tables[g][...], disc_ref[k, g], NN)
        square = value * value + SOFTEN
        inverse = lax.rsqrt(square)
        positive = 0.5 * (value + square * inverse)
        folded = positive[:, :lanes]
        for p0 in range(lanes, paths, lanes):
            folded = folded + positive[:, p0 : p0 + lanes]
        ones = jnp.ones((8, lanes), jnp.float32)
        summed = lax.dot_general(
            ones, folded, NT, precision=lax.Precision.HIGHEST, preferred_element_type=jnp.float32
        )
        expo_ref[k : k + 1, :] = summed[0:1] * scale
        row = weight_ref[k][:, :1] * (0.5 * scale)
        slope_ref[...] = (row * (1.0 + value * inverse)).astype(jnp.bfloat16)
        pull_ref[...] = jnp.zeros_like(pull_ref)
        for g in range(groups):
            back = dot32(slope_ref[...], disc_ref[k, g], NT)
            weighted = back * tables[g][...].astype(jnp.float32)
            pull_ref[g : g + 1, :] = jnp.sum(weighted, axis=0, keepdims=True)
        sens = lax.dot_general(
            pull_ref[...], scaled_ref[k], NN,
            precision=lax.Precision.HIGHEST, preferred_element_type=jnp.float32,
        )
        sens_ref[k] = sens[:groups]


def price(weights, scaled, disc, tables, total_paths):
    slots, groups, cfg, paths = disc.shape
    nodes = scaled.shape[2]
    rows = -(-groups // 8) * 8
    return pl.pallas_call(
        functools.partial(price_kernel, 1.0 / total_paths),
        out_shape=(
            jax.ShapeDtypeStruct((slots, NSETS), jnp.float32),
            jax.ShapeDtypeStruct((slots, groups, nodes), jnp.float32),
        ),
        in_specs=[pl.BlockSpec(memory_space=pltpu.VMEM)] * (3 + groups),
        out_specs=(pl.BlockSpec(memory_space=pltpu.VMEM),) * 2,
        scratch_shapes=[
            pltpu.VMEM((NSETS, paths), jnp.float32),
            pltpu.VMEM((NSETS, paths), jnp.bfloat16),
            pltpu.VMEM((rows, CFG), jnp.float32),
        ],
        cost_estimate=pl.CostEstimate(
            flops=4 * slots * groups * CFG * paths * NSETS,
            bytes_accessed=2 * slots * groups * CFG * paths,
            transcendentals=slots * NSETS * paths,
        ),
        compiler_params=pltpu.CompilerParams(vmem_limit_bytes=VMEM_LIMIT),
        name="price",
    )(weights, scaled, disc, *tables)


def local(curve_store, cash_index, cash_amount, trade_set, date_slot, default_weight):
    groups = lax.axis_size("ccy")
    stations = lax.axis_size("path")
    group_index = lax.axis_index("ccy")
    station = lax.axis_index("path")
    dates = date_slot.shape[0]
    _, slots, nodes, total_paths = curve_store.shape
    paths = total_paths // groups
    share = NSETS // groups

    def swap(array, mask):
        return lax.ppermute(array, "ccy", [(i, i ^ mask) for i in range(groups)])

    flows = (jnp.swapaxes(cash_index[0], 0, 1), jnp.swapaxes(cash_amount[0], 0, 1), trade_set)
    others = {m: tuple(swap(part, m) for part in flows) for m in range(2, groups, 2)}

    def piece(mask):
        begin = (group_index ^ mask) * paths
        return lax.dynamic_slice_in_dim(curve_store[0], begin, paths, 2)

    curves = [piece(0)] + [swap(piece(m), m) for m in range(1, groups)]

    tables = {0: build_table(*flows)}
    for m in others:
        tables[m] = build_table(*others[m])
    for m in list(tables):
        tables[m + 1] = swap(tables[m], 1)
    tables = [tables[m] for m in range(groups)]

    slot_ids = station * slots + jnp.arange(slots, dtype=jnp.int32)
    match = date_slot[None, :] == slot_ids[:, None]
    date_ids = jnp.sum(jnp.where(match, jnp.arange(dates, dtype=jnp.int32)[None, :], 0), axis=1)
    weights = jnp.sum(jnp.where(match[:, :, None], default_weight[None], 0.0), axis=1)
    weights = jnp.broadcast_to(weights[:, :, None], (slots, NSETS, 128))

    disc, scaled = discounts(date_ids, curves)
    expo, sens = price(weights, scaled, disc, tables, total_paths)

    expo = jnp.swapaxes(expo.reshape(slots, groups, share), 0, 1)
    order = group_index ^ jnp.arange(groups)
    pick = (order[:, None] == jnp.arange(groups)[None, :]).astype(jnp.float32)
    sens = jnp.sum(pick[:, :, None, None] * jnp.swapaxes(sens, 0, 1)[None], axis=1)
    payload = jnp.concatenate([expo, sens], axis=2)
    payload = jnp.broadcast_to(payload[:, None], (groups, stations, slots, share + nodes))
    payload = payload.reshape(groups * stations, slots * (share + nodes))
    payload = lax.all_to_all(payload, ("ccy", "path"), 0, 0, tiled=True)
    summed = jnp.sum(payload.reshape(groups, stations * slots, share + nodes), axis=0)
    chosen = (date_slot[:, None] == jnp.arange(stations * slots)[None, :]).astype(jnp.float32)
    rows = jnp.dot(chosen, summed, precision=lax.Precision.HIGHEST)
    return rows[:, :share], rows[:, share:][None]


def solution(mesh):
    in_specs = (
        P("ccy", "path", None, None),
        P("ccy", None, None),
        P("ccy", None, None),
        P("ccy", None),
        P(),
        P(),
    )
    out_specs = (P(None, "ccy"), P("ccy", None, None))
    return jax.shard_map(local, mesh=mesh, in_specs=in_specs, out_specs=out_specs, check_vma=False)
```

time: 762 us -> 114 us (0.15)
  blocking collectives: 382 us -> 11.9 us
  other arithmetic: 187 us -> 1.77 us
  Pallas kernels: 0 us -> 79.4 us
  matrix products: 52 us -> 0.19 us
  local copies, waits for them, and re-layouts: 51.8 us -> 6.36 us
  loops' own time: 40.8 us -> 0 us
  waiting for transfers between devices: 24.2 us -> 5.5 us
  between operations: 14.2 us -> 0.76 us
    psum x16 -> x0, blocking collectives: 293 us -> none  [advance(): exposure_part, sens_part = lax.psum((exposure_part, sens_part), 'path')]
    unnamed x4 -> x0, other arithmetic: 173 us -> none
    all_gather x16 -> x0, blocking collectives: 88.8 us -> none  [advance(): curve_groups = lax.all_gather(curve_now[None], 'ccy', axis=0, tiled=True)]
    pallas_call x0 -> x4, Pallas kernels: none -> 79.4 us  [the longest x2 55.5 us: build_table(): pl.pallas_call(table_kernel, out_shape=jax.ShapeDtypeStruct((NSETS, CFG),...]
    dot_general x64 -> x1, matrix products: 52 us -> 0.19 us  [local(): rows = jnp.dot(chosen, summed, precision=lax.Precision.HIGHEST)]
    another operation x1 -> x0, loops' own time: 40.8 us -> none  [local(): lax.scan(advance, jnp.zeros((), jnp.float32), inputs)]
    dynamic_update_slice x32 -> x0, local copies, waits for them, and re-layouts: 21.1 us -> none  [local(): lax.scan(advance, jnp.zeros((), jnp.float32), inputs)]
    dynamic_slice x48 -> x1, local copies, waits for them, and re-layouts: 19 us -> 0.68 us  [piece(): return lax.dynamic_slice_in_dim(curve_store[0], begin, paths, 2)]
  transfers between devices with their start and end apart: 2 -> 8, of which waited for: 2 -> 2; matrix products, arithmetic and copies ran while one was open for 1% -> 1% of each run, Pallas kernels for 0% -> 55%
where the time goes in v1:
time: 114 us; the launch traced here: 113 us
  Pallas kernels  79.4 us (70%)
  blocking collectives  11.9 us (10%)
  starting transfers between devices  7.41 us (6%)
  local copies, waits for them, and re-layouts  6.36 us (6%)
  waiting for transfers between devices  5.5 us (5%)
  other arithmetic  1.77 us (2%)
    pallas_call x2, Pallas kernels, build_table(): pl.pallas_call(table_kernel, out_shape=jax.ShapeDtypeStruct((NSETS, CFG),...  55.5 us
    pallas_call x1, Pallas kernels, price(): pl.pallas_call(functools.partial(price_kernel, 1.0 / total_paths), out_sh...  16.7 us
    all_to_all x1, blocking collectives, local(): payload = lax.all_to_all(payload, ('ccy', 'path'), 0, 0, tiled=True)  11.9 us
    ppermute x8, starting transfers between devices, swap(): return lax.ppermute(array, 'ccy', [(i, i ^ mask) for i in range(groups)])  7.41 us
    pallas_call x1, Pallas kernels, discounts(): pl.pallas_call(disc_kernel, out_shape=(jax.ShapeDtypeStruct((slots, group...  7.14 us
    ppermute x8, waiting for transfers between devices, swap(): return lax.ppermute(array, 'ccy', [(i, i ^ mask) for i in range(groups)])  5.5 us
    unnamed x22, local copies, waits for them, and re-layouts  2.32 us
  transfers between devices with their start and end apart: 8, of which 2 were waited for; matrix products, arithmetic and copies ran while one was open for 1% of the time, Pallas kernels for 55%

profile of v1, /device:TPU:0, one launch (start us, length us, event | category | flops | bytes accessed | tf_op | source)
XLA Modules:
  0.0 113.3 jit_solution(12615246660205926353)
XLA Ops:
  0.6 3.0 %collective-permute-start.4 = (s32[16,2048]{1,0:T(8,128)}, s32[16,2048]{1,0:T(8,128)S(1)}, u32[]{:S(2)}, u32[]{:S(2)}) collective-permute-start(s32[16,2048]{1,0:T(8,128)} %bitcast.21), channel_id=1, source_target_pairs={{0,16},{8,24},{16,0},{24,8},{1,17},{9,25},{17,1},{25,9},{2,18},{10... | collective-permute-start | bytes 393224 | tf_op jit(solution)/shard_map/ppermute | solution.py:231
  3.7 0.1 collective-permute-start.5
  3.7 1.9 %collective-permute-start.6 = (s32[1,2048]{1,0:T(1,128)}, s32[1,2048]{1,0:T(1,128)S(1)}, u32[]{:S(2)}, u32[]{:S(2)}) collective-permute-start(s32[1,2048]{1,0:T(1,128)} %set_ref.1), channel_id=1, source_target_pairs={{0,16},{8,24},{16,0},{24,8},{1,17},{9,25},{17,1},{25,9},{2,18},{10... | collective-permute-start | bytes 24584 | tf_op jit(solution)/shard_map/ppermute | solution.py:231
  5.7 27.7 %table.2.refs_0_ = bf16[512,1024]{1,0:T(8,128)(2,1)} custom-call(s32[16,2048]{1,0:T(8,128)} %bitcast.22, f32[16,2048]{1,0:T(8,128)} %bitcast.24, s32[1,2048]{1,0:T(1,128)} %set_ref.1), custom_call_target="tpu_custom_call" | custom-call | flops 4294967296 | bytes 2097152 | tf_op jit(solution)/shard_map/table/pallas_call | solution.py:79
  33.4 0.0 copy-start
  33.4 0.0 collective-permute-start.3
  33.4 0.0 copy-start.2
  33.4 0.0 copy-start.1
  33.4 0.0 collective-permute-done.6.set_ref
  33.5 0.0 copy-start.10
  33.5 0.0 collective-permute-done.4.idx_ref
  33.5 0.0 copy-start.5
  33.5 0.0 collective-permute-done.5.amt_ref
  33.5 0.6 copy-done.10
  34.1 0.1 copy-done.5
  34.1 0.0 copy-start.6
  34.1 0.7 copy-done.6
  34.8 27.8 %table.3.refs_2_ = bf16[512,1024]{1,0:T(8,128)(2,1)} custom-call(s32[16,2048]{1,0:T(8,128)} %copy-done.5, f32[16,2048]{1,0:T(8,128)} %copy-done.6, s32[1,2048]{1,0:T(1,128)} %copy-done.10), custom_call_target="tpu_custom_call" | custom-call | flops 4294967296 | bytes 2097152 | tf_op jit(solution)/shard_map/table/pallas_call | solution.py:79
  62.6 0.5 collective-permute-start.7
  63.1 0.0 copy-done
  63.1 0.7 dynamic-slice_bitcast_fusion
  63.8 0.0 collective-permute-start
  63.8 0.1 collective-permute-start.1
  63.9 1.8 %collective-permute-start.2 = (bf16[2,64,512]{2,1,0:T(8,128)(2,1)S(1)}, bf16[2,64,512]{2,1,0:T(8,128)(2,1)S(1)}, u32[]{:S(2)}, u32[]{:S(2)}) collective-permute-start(bf16[2,64,512]{2,1,0:T(8,128)(2,1)S(1)} %get-tuple-element.12), channel_id=1, source_target_pairs={{0,24},{8,16},{16,8},{24,0},{1,25},{9,17},{17,9},{25,1},{2,26},{10... | collective-permute-start | bytes 393224 | tf_op jit(solution)/shard_map/ppermute | solution.py:231
  65.6 0.1 fusion.2
  65.7 0.0 copy-done.2
  65.7 0.7 select_reduce_fusion.1
  66.4 0.0 copy-done.1
  66.4 0.1 select_reduce_fusion
  66.5 0.0 collective-permute-done.refs_1_
  66.5 0.0 copy-start.7
  66.5 3.6 %collective-permute-done.1.refs_2_ = bf16[2,64,512]{2,1,0:T(8,128)(2,1)S(1)} collective-permute-done((bf16[2,64,512]{2,1,0:T(8,128)(2,1)S(1)}, bf16[2,64,512]{2,1,0:T(8,128)(2,1)S(1)}, u32[]{:S(2)}, u32[]{:S(2)}) %collective-permute-start.1) | collective-permute-done | bytes 131104 | tf_op jit(solution)/shard_map/ppermute | solution.py:231
  70.2 0.0 copy-start.8
  70.2 1.8 %collective-permute-done.2.refs_3_ = bf16[2,64,512]{2,1,0:T(8,128)(2,1)S(1)} collective-permute-done((bf16[2,64,512]{2,1,0:T(8,128)(2,1)S(1)}, bf16[2,64,512]{2,1,0:T(8,128)(2,1)S(1)}, u32[]{:S(2)}, u32[]{:S(2)}) %collective-permute-start.2) | collective-permute-done | bytes 131104 | tf_op jit(solution)/shard_map/ppermute | solution.py:231
  72.0 0.0 copy-start.9
  72.0 0.0 copy-done.7
  72.0 0.0 copy-done.8
  72.0 0.6 copy-done.9
  72.6 7.1 %discounts.1 = (bf16[2,4,1024,512]{3,2,1,0:T(8,128)(2,1)}, f32[2,1024,64]{2,1,0:T(8,128)}) custom-call(s32[2]{0:T(128)} %get-tuple-element.10.date_ref, bf16[2,64,512]{2,1,0:T(8,128)(2,1)} %get-tuple-element.14.refs_0_, bf16[2,64,512]{2,1,0:T(8,128)(2,1)} %copy-done.7, bf16[2,64,512]{2,1,0:T(8,128)(2,1)} %copy-done.8, bf16[2,64,512]{2,1,0:T(8,128)(2,1)} %copy-done.9), custom_call_target="tpu_custom_call" | custom-call | flops 2147483648 | bytes 8388608 | tf_op jit(solution)/shard_map/discounts/pallas_call | solution.py:136
  79.8 0.0 collective-permute-done.3.refs_1_
  79.8 0.0 copy-start.3
  79.8 0.0 collective-permute-done.7.refs_3_
  79.8 0.0 copy-start.4
  79.8 1.2 %broadcast_in_dim.41.weight_ref = f32[2,512,128]{2,1,0:T(8,128)} broadcast(f32[2,512]{1,0:T(2,128)S(1)} %select_reduce_fusion), dimensions={0,1} | broadcast | bytes 528384 | tf_op jit(solution)/shard_map/broadcast_in_dim | solution.py:253
  81.0 0.0 copy-done.3
  81.0 0.4 copy-done.4
  81.4 16.7 %price.1 = (f32[2,512]{1,0:T(2,128)}, f32[2,4,64]{2,1,0:T(4,128)}) custom-call(f32[2,512,128]{2,1,0:T(8,128)} %broadcast_in_dim.41.weight_ref, f32[2,1024,64]{2,1,0:T(8,128)} %get-tuple-element.6.scaled_ref, bf16[2,4,1024,512]{3,2,1,0:T(8,128)(2,1)} %get-tuple-element.7.disc_ref, bf16[512,1024]{1,0:T(8,128)(2,1)} %table.2.refs_0_, ...), custom_call_target="tpu_custom_call" | custom-call | flops 8589934592 | bytes 8388608 | tf_op jit(solution)/shard_map/price/pallas_call | solution.py:197
  98.1 0.8 multiply_reduce_fusion
  98.8 0.7 reshape.79
  99.6 0.1 all_to_all.6
  99.7 11.9 %all_to_all.9 = f32[32,1,384]{2,1,0:T(1,128)S(1)} all-to-all(f32[32,1,384]{2,1,0:T(1,128)S(1)} %all_to_all.6), channel_id=1, replica_groups=mesh['ccy'=4,'path'=8] {'ccy','path'}, dimensions={0} | all-to-all | bytes 98304 | tf_op jit(solution)/shard_map/all_to_all | solution.py:265
  111.7 0.1 reduce
  111.8 0.1 reshape.80
  111.9 0.2 fusion
  112.1 0.6 slice.8
  112.7 0.6 slice_bitcast_fusion
  (7 shorter events, 0.1 us)
Async XLA Ops:
  0.6 32.8 %collective-permute-start.4 = (s32[16,2048]{1,0:T(8,128)}, s32[16,2048]{1,0:T(8,128)S(1)}, u32[]{:S(2)}, u32[]{:S(2)}) collective-permute-start(s32[16,2048]{1,0:T(8,128)} %bitcast.21), channel_id=1, source_target_pairs={{0,16},{8,24},{16,0},{24,8},{1,17},{9,25},{17,1},{25,9},{2,18},{10... | collective-permute-start | bytes 393224 | tf_op jit(solution)/shard_map/ppermute | solution.py:231
  3.7 29.8 %collective-permute-start.5 = (f32[16,2048]{1,0:T(8,128)}, f32[16,2048]{1,0:T(8,128)S(1)}, u32[]{:S(2)}, u32[]{:S(2)}) collective-permute-start(f32[16,2048]{1,0:T(8,128)} %bitcast.23), channel_id=1, source_target_pairs={{0,16},{8,24},{16,0},{24,8},{1,17},{9,25},{17,1},{25,9},{2,18},{10... | collective-permute-start | bytes 393224 | tf_op jit(solution)/shard_map/ppermute | solution.py:231
  3.7 29.7 %collective-permute-start.6 = (s32[1,2048]{1,0:T(1,128)}, s32[1,2048]{1,0:T(1,128)S(1)}, u32[]{:S(2)}, u32[]{:S(2)}) collective-permute-start(s32[1,2048]{1,0:T(1,128)} %set_ref.1), channel_id=1, source_target_pairs={{0,16},{8,24},{16,0},{24,8},{1,17},{9,25},{17,1},{25,9},{2,18},{10... | collective-permute-start | bytes 24584 | tf_op jit(solution)/shard_map/ppermute | solution.py:231
  33.4 29.7 %copy-start = (bf16[1,2,64,2048]{3,2,1,0:T(8,128)(2,1)S(1)}, bf16[1,2,64,2048]{3,2,1,0:T(8,128)(2,1)}, u32[]{:S(2)}) copy-start(bf16[1,2,64,2048]{3,2,1,0:T(8,128)(2,1)} %param.6) | copy-start | bytes 1572868
  33.4 46.4 %collective-permute-start.3 = (bf16[512,1024]{1,0:T(8,128)(2,1)}, bf16[512,1024]{1,0:T(8,128)(2,1)S(1)}, u32[]{:S(2)}, u32[]{:S(2)}) collective-permute-start(bf16[512,1024]{1,0:T(8,128)(2,1)} %table.2.refs_0_), channel_id=1, source_target_pairs={{0,8},{8,0},{16,24},{24,16},{1,9},{9,1},{17,25},{25,17},{2,10},{10... | collective-permute-start | bytes 3145736 | tf_op jit(solution)/shard_map/ppermute | solution.py:231
  33.4 32.3 %copy-start.2 = (s32[16]{0:T(128)S(1)}, s32[16]{0:T(128)}, u32[]{:S(2)}) copy-start(s32[16]{0:T(128)} %param.10) | copy-start | bytes 196
  33.4 33.0 %copy-start.1 = (f32[16,512]{1,0:T(8,128)S(1)}, f32[16,512]{1,0:T(8,128)}, u32[]{:S(2)}) copy-start(f32[16,512]{1,0:T(8,128)} %param.11) | copy-start | bytes 98308
  33.5 0.6 copy-start.10
  33.5 0.7 copy-start.5
  34.1 0.7 copy-start.6
  62.6 17.2 %collective-permute-start.7 = (bf16[512,1024]{1,0:T(8,128)(2,1)}, bf16[512,1024]{1,0:T(8,128)(2,1)S(1)}, u32[]{:S(2)}, u32[]{:S(2)}) collective-permute-start(bf16[512,1024]{1,0:T(8,128)(2,1)} %table.3.refs_2_), channel_id=1, source_target_pairs={{0,8},{8,0},{16,24},{24,16},{1,9},{9,1},{17,25},{25,17},{2,10},{10... | collective-permute-start | bytes 3145736 | tf_op jit(solution)/shard_map/ppermute | solution.py:231
  63.8 2.7 %collective-permute-start = (bf16[2,64,512]{2,1,0:T(8,128)(2,1)S(1)}, bf16[2,64,512]{2,1,0:T(8,128)(2,1)S(1)}, u32[]{:S(2)}, u32[]{:S(2)}) collective-permute-start(bf16[2,64,512]{2,1,0:T(8,128)(2,1)S(1)} %get-tuple-element.13), channel_id=1, source_target_pairs={{0,8},{8,0},{16,24},{24,16},{1,9},{9,1},{17,25},{25,17},{2,10},{10... | collective-permute-start | bytes 393224 | tf_op jit(solution)/shard_map/ppermute | solution.py:231
  63.8 6.4 %collective-permute-start.1 = (bf16[2,64,512]{2,1,0:T(8,128)(2,1)S(1)}, bf16[2,64,512]{2,1,0:T(8,128)(2,1)S(1)}, u32[]{:S(2)}, u32[]{:S(2)}) collective-permute-start(bf16[2,64,512]{2,1,0:T(8,128)(2,1)S(1)} %get-tuple-element.15), channel_id=1, source_target_pairs={{0,16},{8,24},{16,0},{24,8},{1,17},{9,25},{17,1},{25,9},{2,18},{10... | collective-permute-start | bytes 393224 | tf_op jit(solution)/shard_map/ppermute | solution.py:231
  63.9 8.1 %collective-permute-start.2 = (bf16[2,64,512]{2,1,0:T(8,128)(2,1)S(1)}, bf16[2,64,512]{2,1,0:T(8,128)(2,1)S(1)}, u32[]{:S(2)}, u32[]{:S(2)}) collective-permute-start(bf16[2,64,512]{2,1,0:T(8,128)(2,1)S(1)} %get-tuple-element.12), channel_id=1, source_target_pairs={{0,24},{8,16},{16,8},{24,0},{1,25},{9,17},{17,9},{25,1},{2,26},{10... | collective-permute-start | bytes 393224 | tf_op jit(solution)/shard_map/ppermute | solution.py:231
  66.5 5.5 %copy-start.7 = (bf16[2,64,512]{2,1,0:T(8,128)(2,1)}, bf16[2,64,512]{2,1,0:T(8,128)(2,1)S(1)}, u32[]{:S(2)}) copy-start(bf16[2,64,512]{2,1,0:T(8,128)(2,1)S(1)} %collective-permute-done.refs_1_) | copy-start | bytes 393220
  70.2 1.8 %copy-start.8 = (bf16[2,64,512]{2,1,0:T(8,128)(2,1)}, bf16[2,64,512]{2,1,0:T(8,128)(2,1)S(1)}, u32[]{:S(2)}) copy-start(bf16[2,64,512]{2,1,0:T(8,128)(2,1)S(1)} %collective-permute-done.1.refs_2_) | copy-start | bytes 393220
  72.0 0.7 copy-start.9
  79.8 1.2 %copy-start.3 = (bf16[512,1024]{1,0:T(8,128)(2,1)}, bf16[512,1024]{1,0:T(8,128)(2,1)S(1)}, u32[]{:S(2)}) copy-start(bf16[512,1024]{1,0:T(8,128)(2,1)S(1)} %collective-permute-done.3.refs_1_) | copy-start | bytes 3145732
  79.8 1.6 %copy-start.4 = (bf16[512,1024]{1,0:T(8,128)(2,1)}, bf16[512,1024]{1,0:T(8,128)(2,1)S(1)}, u32[]{:S(2)}) copy-start(bf16[512,1024]{1,0:T(8,128)(2,1)S(1)} %collective-permute-done.7.refs_3_) | copy-start | bytes 3145732

commit v2 on v0

v2 whole, which is shorter than its diff:
```python
import functools
import math

import jax
import jax.numpy as jnp
from jax import lax
from jax.experimental import pallas as pl
from jax.experimental.pallas import tpu as pltpu
from jax.sharding import PartitionSpec as P


CFG = 1024
NSETS = 512
SOFTEN = 0.04
HORIZON = 32.0
LOG2E = math.log2(math.e)
LANES = 128
SUB = 16
WIDE = 256

NT = (((1,), (1,)), ((), ()))
NN = (((1,), (0,)), ((), ()))
TN = (((0,), (0,)), ((), ()))
VM = pl.BlockSpec(memory_space=pltpu.VMEM)
SM = pl.BlockSpec(memory_space=pltpu.SMEM)


def dot16(a, b, dims):
    return lax.dot_general(a, b, dims, preferred_element_type=jnp.float32)


def dot_full(a, b, dims):
    return lax.dot_general(
        a, b, dims, precision=lax.Precision.HIGHEST, preferred_element_type=jnp.float32
    )


def join(ref, blocks):
    return jnp.concatenate([ref[b] for b in blocks], axis=1)


def table_kernel(flow_ref, out_ref, date_t, high_t, one_hot, slot_a, slot_b, acc_ref):
    ncf, trades = flow_ref.shape[0] // 2, flow_ref.shape[1]
    blocks = trades // LANES
    row_ids = lax.broadcasted_iota(jnp.int32, (NSETS // SUB, SUB, LANES), 0) * SUB
    row_ids = (row_ids + lax.broadcasted_iota(jnp.int32, row_ids.shape, 1)).astype(jnp.int16)
    unit = jnp.ones((NSETS // SUB, SUB, LANES), jnp.bfloat16)

    def spread(row):
        return jnp.broadcast_to(row, (SUB, LANES))

    def prepare(b, carry):
        cols = pl.ds(pl.multiple_of(b * LANES, LANES), LANES)
        code = flow_ref[:ncf, cols].astype(jnp.int32)
        amount = flow_ref[ncf:, cols]
        date = code & (CFG - 1)
        sets = lax.shift_right_logical(code[0:1, :], CFG.bit_length() - 1)
        total = jnp.zeros((ncf, LANES), jnp.float32)
        for k in range(ncf):
            same = date == date[k : k + 1, :]
            total = total + jnp.where(same, amount[k : k + 1, :], 0.0)
        for k in range(ncf):
            rows = slice(k * SUB, (k + 1) * SUB)
            date_t[b, rows, :] = spread(date[k : k + 1, :]).astype(jnp.int16)
            high_t[b, rows, :] = spread(total[k : k + 1, :]).astype(jnp.bfloat16)
        mine = spread(sets).astype(jnp.int16)[None]
        chosen = jnp.where(row_ids == mine, unit, jnp.zeros_like(unit))
        one_hot[b] = chosen.reshape(NSETS, LANES)
        return carry

    lax.fori_loop(0, blocks, prepare, 0)

    chunk, tiles = 8, 8
    step = tiles * SUB
    parts = CFG // WIDE
    base = lax.broadcasted_iota(jnp.int32, (tiles, SUB, LANES), 0) * SUB
    base = base + lax.broadcasted_iota(jnp.int32, (tiles, SUB, LANES), 1)
    slots = (slot_a, slot_b)

    def fill(slot, part, b):
        for r in range(0, WIDE, step):
            want = (base + (part * WIDE + r)).astype(jnp.int16)
            acc = jnp.zeros((tiles, SUB, LANES), jnp.bfloat16)
            for k in range(ncf):
                rows = slice(k * SUB, (k + 1) * SUB)
                acc = jnp.where(want == date_t[b, rows, :][None], high_t[b, rows, :][None], acc)
            slot[b, r : r + step, :] = acc.reshape(step, LANES)

    for part in range(parts + 1):
        target, source = slots[part % 2], slots[(part + 1) % 2]
        if part > 0:
            acc_ref[...] = jnp.zeros_like(acc_ref)

        def body(q, carry, part=part, target=target, source=source):
            mine = [q * chunk + i for i in range(chunk)]
            if part > 0:
                acc_ref[...] += dot16(join(one_hot, mine), join(source, mine), NT)
            if part < parts:
                for b in mine:
                    fill(target, part, b)
            return carry

        lax.fori_loop(0, blocks // chunk, body, 0)
        if part > 0:
            block = acc_ref[...].astype(jnp.bfloat16)
            for i in range(WIDE // LANES):
                place = (part - 1) * (WIDE // LANES) + i
                out_ref[place] = block[:, i * LANES : (i + 1) * LANES]


def build_table(flows):
    ncf, trades = flows.shape[0] // 2, flows.shape[1]
    blocks = trades // LANES
    return pl.pallas_call(
        table_kernel,
        out_shape=jax.ShapeDtypeStruct((CFG // LANES, NSETS, LANES), jnp.bfloat16),
        in_specs=[VM],
        out_specs=VM,
        scratch_shapes=[
            pltpu.VMEM((blocks, ncf * SUB, LANES), jnp.int16),
            pltpu.VMEM((blocks, ncf * SUB, LANES), jnp.bfloat16),
            pltpu.VMEM((blocks, NSETS, LANES), jnp.bfloat16),
            pltpu.VMEM((blocks, WIDE, LANES), jnp.bfloat16),
            pltpu.VMEM((blocks, WIDE, LANES), jnp.bfloat16),
            pltpu.VMEM((NSETS, WIDE), jnp.float32),
        ],
        cost_estimate=pl.CostEstimate(
            flops=4 * trades * NSETS * CFG, bytes_accessed=2**21, transcendentals=0
        ),
        compiler_params=pltpu.CompilerParams(vmem_limit_bytes=16 * 2**20),
    )(flows)


def date_of(slot_ref, station_ref, slots, k):
    mine = station_ref[0] * slots + k
    date, found = 0, 0
    for d in range(slot_ref.shape[0]):
        hit = slot_ref[d] == mine
        date = jnp.where(hit, d, date)
        found = jnp.where(hit, 1, found)
    return date, found


def disc_kernel(groups, slot_ref, station_ref, *refs):
    curves, (disc_ref, scaled_ref, rhs) = refs[:groups], refs[groups:]
    slots, nodes, paths = curves[0].shape
    depth = rhs.shape[0]
    rhs[3 * nodes :, :] = jnp.ones((depth - 3 * nodes, paths), jnp.bfloat16)
    for k in range(slots):
        date, _ = date_of(slot_ref, station_ref, slots, k)
        start = 0.5 * (date.astype(jnp.float32) + 1.0)
        grid = lax.broadcasted_iota(jnp.int32, (CFG, nodes), 0).astype(jnp.float32)
        remain = HORIZON * (grid + 1.0) / CFG - start
        node = lax.broadcasted_iota(jnp.int32, (CFG, nodes), 1).astype(jnp.float32)
        tenor = HORIZON * (node + 1.0) / nodes
        clipped = jnp.clip(remain, HORIZON / nodes, HORIZON)
        weight = jnp.maximum(0.0, 1.0 - jnp.abs(clipped - tenor) * (nodes / HORIZON))
        scaled = weight * (remain * (-LOG2E))
        scaled_ref[k] = weight * -remain
        high = scaled.astype(jnp.bfloat16)
        rest = scaled - high.astype(jnp.float32)
        mid = rest.astype(jnp.bfloat16)
        low = (rest - mid.astype(jnp.float32)).astype(jnp.bfloat16)
        dead = jnp.where((node == 0.0) & (remain <= 0.0), -1e30, 0.0).astype(jnp.bfloat16)
        left = jnp.concatenate([high, mid, low, dead], axis=1)
        for g in range(groups):
            part = curves[g][k]
            for copy in range(3):
                rhs[copy * nodes : (copy + 1) * nodes, :] = part
            for p0 in range(0, paths, WIDE):
                block = jnp.exp2(dot16(left, rhs[:, p0 : p0 + WIDE], NN)).astype(jnp.bfloat16)
                for i in range(WIDE // LANES):
                    disc_ref[k, g, p0 // LANES + i] = block[:, i * LANES : (i + 1) * LANES]


def discounts(date_slot, station, curves):
    slots, nodes, paths = curves[0].shape
    groups = len(curves)
    return pl.pallas_call(
        functools.partial(disc_kernel, groups),
        out_shape=(
            jax.ShapeDtypeStruct((slots, groups, paths // LANES, CFG, LANES), jnp.bfloat16),
            jax.ShapeDtypeStruct((slots, CFG, nodes), jnp.float32),
        ),
        in_specs=[SM, SM] + [VM] * groups,
        out_specs=(VM, VM),
        scratch_shapes=[pltpu.VMEM((4 * nodes, paths), jnp.bfloat16)],
        cost_estimate=pl.CostEstimate(
            flops=2 * slots * groups * CFG * paths * 4 * nodes,
            bytes_accessed=2 * slots * groups * CFG * paths,
            transcendentals=slots * groups * CFG * paths,
        ),
        compiler_params=pltpu.CompilerParams(
            vmem_limit_bytes=8 * 2**20 + 3 * slots * groups * CFG * paths
        ),
        name="discounts",
    )(date_slot, station, *curves)


def price_kernel(stations, scale, slot_ref, station_ref, member_ref, weight_ref, scaled_ref,
                 disc_ref, *refs):
    groups = disc_ref.shape[1]
    tables = refs[:groups]
    out_ref, slope_ref, expo_ref, pull_ref, sens_ref = refs[groups:]
    slots = disc_ref.shape[0]
    pblocks = disc_ref.shape[2]
    cblocks = CFG // LANES
    nodes = scaled_ref.shape[2]
    share = NSETS // groups
    wide = WIDE // LANES
    lead = (lax.broadcasted_iota(jnp.int32, (8, LANES), 0) == 0).astype(jnp.float32)
    pull_ref[...] = jnp.zeros_like(pull_ref)
    for k in range(slots):
        date, found = date_of(slot_ref, station_ref, slots, k)
        row = weight_ref[pl.ds(date, 1), :] * (0.5 * scale) * found.astype(jnp.float32)
        column = dot_full(jnp.broadcast_to(row, (8, NSETS)), lead, TN)
        folded = jnp.zeros((NSETS, LANES), jnp.float32)
        left = jnp.concatenate([join(tables[g], range(cblocks)) for g in range(groups)], axis=1)
        for p0 in range(0, pblocks, wide):
            right = jnp.concatenate(
                [join(disc_ref.at[k, g], range(p0, p0 + wide)) for g in range(groups)], axis=0
            )
            value = dot16(left, right, NN)
            for i in range(wide):
                part = value[:, i * LANES : (i + 1) * LANES]
                square = part * part + SOFTEN
                inverse = lax.rsqrt(square)
                folded = folded + (part + square * inverse)
                slope = column + column * (part * inverse)
                slope_ref[p0 + i] = slope.astype(jnp.bfloat16)
        summed = dot_full(jnp.ones((8, LANES), jnp.float32), folded, NT)
        expo_ref[k : k + 1, :] = summed[0:1] * (0.5 * scale)
        slope_all = join(slope_ref, range(pblocks))
        for g in range(groups):
            for c0 in range(0, cblocks, wide):
                right = jnp.concatenate(
                    [disc_ref[k, g, p, c0 * LANES : (c0 + wide) * LANES, :] for p in range(pblocks)],
                    axis=1,
                )
                back = dot16(slope_all, right, NT)
                for i in range(wide):
                    cash = tables[g][c0 + i].astype(jnp.float32)
                    pull = jnp.sum(back[:, i * LANES : (i + 1) * LANES] * cash, axis=0)
                    cols = slice((c0 + i) * LANES, (c0 + i + 1) * LANES)
                    pull_ref[g : g + 1, cols] = pull[None]
        sens_ref[k] = dot_full(pull_ref[...], scaled_ref[k], NN)
    for g in range(groups):
        rows = slice(g * stations, (g + 1) * stations)
        mask = member_ref[0] ^ g
        for k in range(slots):
            part = expo_ref[k : k + 1, g * share : (g + 1) * share]
            out_ref[rows, k * share : (k + 1) * share] = jnp.broadcast_to(part, (stations, share))
        line = jnp.concatenate([sens_ref[k, pl.ds(mask, 1), :] for k in range(slots)], axis=1)
        out_ref[rows, slots * share :] = jnp.broadcast_to(line, (stations, slots * nodes))


def price(date_slot, station, member, weights, scaled, disc, tables, stations, total_paths):
    slots, groups, pblocks = disc.shape[:3]
    nodes = scaled.shape[2]
    paths = pblocks * LANES
    rows = -(-groups // 8) * 8
    return pl.pallas_call(
        functools.partial(price_kernel, stations, 1.0 / total_paths),
        out_shape=jax.ShapeDtypeStruct(
            (groups * stations, slots * (NSETS // groups + nodes)), jnp.float32
        ),
        in_specs=[SM] * 3 + [VM] * (3 + groups),
        out_specs=VM,
        scratch_shapes=[
            pltpu.VMEM((pblocks, NSETS, LANES), jnp.bfloat16),
            pltpu.VMEM((slots, NSETS), jnp.float32),
            pltpu.VMEM((rows, CFG), jnp.float32),
            pltpu.VMEM((slots, rows, nodes), jnp.float32),
        ],
        cost_estimate=pl.CostEstimate(
            flops=4 * slots * groups * CFG * paths * NSETS,
            bytes_accessed=2 * slots * groups * CFG * paths,
            transcendentals=slots * NSETS * paths,
        ),
        compiler_params=pltpu.CompilerParams(
            vmem_limit_bytes=16 * 2**20 + 3 * slots * groups * CFG * paths // 2
        ),
        name="price",
    )(date_slot, station, member, weights, scaled, disc, *tables)


def collect_kernel(groups, slots, nodes, slot_ref, got_ref, expo_ref, sens_ref, sum_ref):
    stations = sum_ref.shape[0]
    dates, share = expo_ref.shape
    total = got_ref[:stations]
    for g in range(1, groups):
        total = total + got_ref[g * stations : (g + 1) * stations]
    sum_ref[...] = total
    for d in range(dates):
        slot = slot_ref[d]
        line = sum_ref[pl.ds(slot // slots, 1), :]
        expo, sens = line[:, :share], line[:, slots * share : slots * share + nodes]
        for k in range(1, slots):
            here = slot % slots == k
            begin = slots * share + k * nodes
            expo = jnp.where(here, line[:, k * share : (k + 1) * share], expo)
            sens = jnp.where(here, line[:, begin : begin + nodes], sens)
        expo_ref[d : d + 1, :] = expo
        sens_ref[d : d + 1, :] = sens


def collect(date_slot, got, groups, slots, nodes):
    dates = date_slot.shape[0]
    share = NSETS // groups
    return pl.pallas_call(
        functools.partial(collect_kernel, groups, slots, nodes),
        out_shape=(
            jax.ShapeDtypeStruct((dates, share), jnp.float32),
            jax.ShapeDtypeStruct((dates, nodes), jnp.float32),
        ),
        in_specs=[SM, VM],
        out_specs=(VM, VM),
        scratch_shapes=[pltpu.VMEM((got.shape[0] // groups, got.shape[1]), jnp.float32)],
        name="collect",
    )(date_slot, got)


def local(curve_store, cash_index, cash_amount, trade_set, date_slot, default_weight):
    groups = lax.axis_size("ccy")
    stations = lax.axis_size("path")
    member = lax.axis_index("ccy").astype(jnp.int32)
    station = lax.axis_index("path").astype(jnp.int32)
    _, slots, nodes, total_paths = curve_store.shape
    paths = total_paths // groups

    def swap(array, mask):
        return lax.ppermute(array, "ccy", [(i, i ^ mask) for i in range(groups)])

    code = jnp.swapaxes(cash_index[0], 0, 1) + CFG * trade_set
    flows = jnp.concatenate([code.astype(jnp.float32), jnp.swapaxes(cash_amount[0], 0, 1)], axis=0)
    others = {m: swap(flows, m) for m in range(2, groups, 2)}

    def piece(mask):
        begin = (member ^ mask) * paths
        return lax.dynamic_slice_in_dim(curve_store[0], begin, paths, 2)

    curves = [piece(0)] + [swap(piece(m), m) for m in range(1, groups)]

    tables = {0: build_table(flows)}
    for m in others:
        tables[m] = build_table(others[m])
    for m in list(tables):
        tables[m + 1] = swap(tables[m], 1)
    tables = [tables[m] for m in range(groups)]

    disc, scaled = discounts(date_slot, station[None], curves)
    payload = price(
        date_slot, station[None], member[None], default_weight, scaled, disc, tables,
        stations, total_paths,
    )
    got = lax.all_to_all(payload, ("ccy", "path"), 0, 0, tiled=True)
    expo, sens = collect(date_slot, got, groups, slots, nodes)
    return expo, sens[None]


def solution(mesh):
    in_specs = (
        P("ccy", "path", None, None),
        P("ccy", None, None),
        P("ccy", None, None),
        P("ccy", None),
        P(),
        P(),
    )
    out_specs = (P(None, "ccy"), P("ccy", None, None))
    return jax.shard_map(local, mesh=mesh, in_specs=in_specs, out_specs=out_specs, check_vma=False)
```

time: 762 us -> 64 us (0.08)
  blocking collectives: 382 us -> 12 us
  other arithmetic: 187 us -> 2.57 us
  matrix products: 52 us -> 0 us
  local copies, waits for them, and re-layouts: 51.8 us -> 3.3 us
  loops' own time: 40.8 us -> 0 us
  Pallas kernels: 0 us -> 32.9 us
  waiting for transfers between devices: 24.2 us -> 6.67 us
  between operations: 14.2 us -> 0.72 us
    psum x16 -> x0, blocking collectives: 293 us -> none  [advance(): exposure_part, sens_part = lax.psum((exposure_part, sens_part), 'path')]
    unnamed x4 -> x0, other arithmetic: 173 us -> none
    all_gather x16 -> x0, blocking collectives: 88.8 us -> none  [advance(): curve_groups = lax.all_gather(curve_now[None], 'ccy', axis=0, tiled=True)]
    dot_general x64 -> x0, matrix products: 52 us -> none  [the longest x16 21.4 us: advance(): jnp.einsum('gpc,gcs->ps', discount_all.astype(jnp.bfloat16), cash_all, pr...]
    another operation x1 -> x0, loops' own time: 40.8 us -> none  [local(): lax.scan(advance, jnp.zeros((), jnp.float32), inputs)]
    pallas_call x0 -> x5, Pallas kernels: none -> 32.9 us  [the longest x2 14.8 us: build_table(): pl.pallas_call(table_kernel, out_shape=jax.ShapeDtypeStruct((CFG // LANES...]
    dynamic_update_slice x32 -> x0, local copies, waits for them, and re-layouts: 21.1 us -> none  [local(): lax.scan(advance, jnp.zeros((), jnp.float32), inputs)]
    dynamic_slice x48 -> x1, local copies, waits for them, and re-layouts: 19 us -> 1.85 us  [piece(): return lax.dynamic_slice_in_dim(curve_store[0], begin, paths, 2)]
  transfers between devices with their start and end apart: 2 -> 6, of which waited for: 2 -> 2; matrix products, arithmetic and copies ran while one was open for 1% -> 3% of each run, Pallas kernels for 0% -> 29%
where the time goes in v2:
time: 64 us; the launch traced here: 63.6 us
  Pallas kernels  32.9 us (51%)
  blocking collectives  12 us (19%)
  waiting for transfers between devices  6.67 us (10%)
  starting transfers between devices  5.51 us (9%)
  local copies, waits for them, and re-layouts  3.3 us (5%)
  other arithmetic  2.57 us (4%)
  between operations  0.72 us (1%)
    pallas_call x2, Pallas kernels, build_table(): pl.pallas_call(table_kernel, out_shape=jax.ShapeDtypeStruct((CFG // LANES...  14.8 us
    pallas_call x1, Pallas kernels, price(): pl.pallas_call(functools.partial(price_kernel, stations, 1.0 / total_path...  12.8 us
    all_to_all x1, blocking collectives, local(): got = lax.all_to_all(payload, ('ccy', 'path'), 0, 0, tiled=True)  12 us
    ppermute x6, waiting for transfers between devices, swap(): return lax.ppermute(array, 'ccy', [(i, i ^ mask) for i in range(groups)])  6.67 us
    ppermute x6, starting transfers between devices, swap(): return lax.ppermute(array, 'ccy', [(i, i ^ mask) for i in range(groups)])  5.51 us
    pallas_call x1, Pallas kernels, discounts(): pl.pallas_call(functools.partial(disc_kernel, groups), out_shape=(jax.Sha...  3.72 us
    dynamic_slice x1, local copies, waits for them, and re-layouts, piece(): return lax.dynamic_slice_in_dim(curve_store[0], begin, paths, 2)  1.85 us
    pallas_call x1, Pallas kernels, collect(): pl.pallas_call(functools.partial(collect_kernel, groups, slots, nodes), o...  1.58 us
  transfers between devices with their start and end apart: 6, of which 2 were waited for; matrix products, arithmetic and copies ran while one was open for 3% of the time, Pallas kernels for 29%

profile of v2, /device:TPU:0, one launch (start us, length us, event | category | flops | bytes accessed | tf_op | source)
XLA Modules:
  0.0 63.6 jit_solution(4490255538019074223)
XLA Ops:
  0.6 0.7 %broadcast_multiply_fusion = s32[1,2048]{1,0:T(1,128)S(1)} fusion(s32[1,2048]{1,0:T(1,128)} %param.9), kind=kLoop, calls=%fused_computation.9 | loop fusion | flops 2048 | bytes 16384 | tf_op jit(solution)/shard_map/mul | solution.py:334
  1.3 0.9 %fusion.1 = f32[16,2048]{1,0:T(8,128)S(1)} fusion(s32[1,2048,16]{1,2,0:T(8,128)} %param.7, s32[2048]{0:T(1024)S(1)} %bitcast.30), kind=kLoop, calls=%fused_computation.3 | loop fusion | flops 65536 | bytes 270336 | tf_op jit(solution)/shard_map/convert_element_type | solution.py:335
  2.3 0.9 %pad_maximum_fusion.flow_ref = f32[32,2048]{1,0:T(8,128)S(1)} fusion(f32[16,2048]{1,0:T(8,128)} %bitcast.29, f32[16,2048]{1,0:T(8,128)S(1)} %fusion.1), kind=kLoop, calls=%fused_computation | loop fusion | flops 65536 | bytes 524288 | tf_op jit(solution)/shard_map/concatenate | solution.py:335
  3.2 3.0 %collective-permute-start.4 = (f32[32,2048]{1,0:T(8,128)S(1)}, f32[32,2048]{1,0:T(8,128)S(1)}, u32[]{:S(2)}, u32[]{:S(2)}) collective-permute-start(f32[32,2048]{1,0:T(8,128)S(1)} %pad_maximum_fusion.flow_ref), channel_id=1, source_target_pairs={{0,16},{8,24},{16,0},{24,8},{1,17},{9,25},{17,1},{25,9},{2,18},{10... | collective-permute-start | bytes 786440 | tf_op jit(solution)/shard_map/ppermute | solution.py:332
  6.2 7.3 %shard_map.77.refs_0_ = bf16[8,512,128]{2,1,0:T(8,128)(2,1)S(1)} custom-call(f32[32,2048]{1,0:T(8,128)S(1)} %pad_maximum_fusion.flow_ref), custom_call_target="tpu_custom_call" | custom-call | flops 4294967296 | bytes 2097152 | tf_op jit(solution)/shard_map/pallas_call | solution.py:114
  13.6 0.0 copy-start
  13.6 0.1 collective-permute-start.3
  13.7 0.0 collective-permute-done.4.flow_ref
  13.7 7.5 %shard_map.78.refs_2_ = bf16[8,512,128]{2,1,0:T(8,128)(2,1)S(1)} custom-call(f32[32,2048]{1,0:T(8,128)S(1)} %collective-permute-done.4.flow_ref), custom_call_target="tpu_custom_call" | custom-call | flops 4294967296 | bytes 2097152 | tf_op jit(solution)/shard_map/pallas_call | solution.py:114
  21.2 0.6 collective-permute-start.5
  21.7 1.9 %dynamic-slice_bitcast_fusion = (bf16[2,64,512]{2,1,0:T(8,128)(2,1)}, bf16[2,64,512]{2,1,0:T(8,128)(2,1)}, bf16[2,64,512]{2,1,0:T(8,128)(2,1)S(1)}, bf16[2,64,512]{2,1,0:T(8,128)(2,1)}) fusion(bf16[1,2,64,2048]{3,2,1,0:T(8,128)(2,1)} %param.6, s32[]{:T(128)S(6)} %select_n.15, s32[]{:T(128)S(6)} %select_n.13, s32[]{:T(128)S(6)} %select_n.12, s32[]{:T(128)S(6)} %select_n.14), kind=kLoop, calls=%fused_computation.4 | loop fusion | bytes 1048592 | tf_op jit(solution)/shard_map/dynamic_slice | solution.py:340
  23.6 0.1 collective-permute-start
  23.6 0.6 collective-permute-start.1
  24.2 1.2 %collective-permute-start.2 = (bf16[2,64,512]{2,1,0:T(8,128)(2,1)}, bf16[2,64,512]{2,1,0:T(8,128)(2,1)}, u32[]{:S(2)}, u32[]{:S(2)}) collective-permute-start(bf16[2,64,512]{2,1,0:T(8,128)(2,1)} %get-tuple-element.10), channel_id=1, source_target_pairs={{0,24},{8,16},{16,8},{24,0},{1,25},{9,17},{17,9},{25,1},{2,26},{10... | collective-permute-start | bytes 393224 | tf_op jit(solution)/shard_map/ppermute | solution.py:332
  25.4 0.0 collective-permute-done.refs_1_
  25.4 4.8 %collective-permute-done.1.refs_2_ = bf16[2,64,512]{2,1,0:T(8,128)(2,1)S(1)} collective-permute-done((bf16[2,64,512]{2,1,0:T(8,128)(2,1)}, bf16[2,64,512]{2,1,0:T(8,128)(2,1)S(1)}, u32[]{:S(2)}, u32[]{:S(2)}) %collective-permute-start.1) | collective-permute-done | bytes 131104 | tf_op jit(solution)/shard_map/ppermute | solution.py:332
  30.2 1.9 %collective-permute-done.2.refs_3_ = bf16[2,64,512]{2,1,0:T(8,128)(2,1)} collective-permute-done((bf16[2,64,512]{2,1,0:T(8,128)(2,1)}, bf16[2,64,512]{2,1,0:T(8,128)(2,1)}, u32[]{:S(2)}, u32[]{:S(2)}) %collective-permute-start.2) | collective-permute-done | bytes 131104 | tf_op jit(solution)/shard_map/ppermute | solution.py:332
  32.1 0.0 copy-done
  32.1 3.7 %discounts.1 = (bf16[2,4,4,1024,128]{4,3,2,1,0:T(8,128)(2,1)S(1)}, f32[2,1024,64]{2,1,0:T(8,128)S(1)}) custom-call(s32[16]{0:T(128)S(1)} %copy-done, s32[1]{0:T(128)} %bitcast.station_ref, bf16[2,64,512]{2,1,0:T(8,128)(2,1)S(1)} %get-tuple-element.12.refs_0_, bf16[2,64,512]{2,1,0:T(8,128)(2,1)S(1)} %collective-permute-done.refs_1_, ...), custom_call_target="tpu_custom_call" | custom-call | flops 2147483648 | bytes 8388608 | tf_op jit(solution)/shard_map/discounts/pallas_call | solution.py:179
  35.8 0.0 collective-permute-done.3.refs_1_
  35.8 0.0 collective-permute-done.5.refs_3_
  35.9 0.0 copy-start.1
  35.9 0.7 %copy-done.1 = f32[16,512]{1,0:T(8,128)S(1)} copy-done((f32[16,512]{1,0:T(8,128)S(1)}, f32[16,512]{1,0:T(8,128)}, u32[]{:S(2)}) %copy-start.1) | copy-done | bytes 32792
  36.6 12.8 %price.1 = f32[32,384]{1,0:T(8,128)S(1)} custom-call(s32[16]{0:T(128)S(1)} %copy-done, s32[1]{0:T(128)} %bitcast.station_ref, s32[1]{0:T(128)} %bitcast.1.member_ref, f32[16,512]{1,0:T(8,128)S(1)} %copy-done.1, f32[2,1024,64]{2,1,0:T(8,128)S(1)} %get-tuple-element.6.scaled_ref, bf16[2,4,4,1024,128]{4,3,2,1,0:T(8,128)(2,1)S(1)} %get-tuple-element.7.disc_ref, ...), custom_call_target="tpu_custom_call" | custom-call | flops 8589934592 | bytes 8388608 | tf_op jit(solution)/shard_map/price/pallas_call | solution.py:262
  49.4 0.1 copy.8
  49.5 12.0 %all_to_all.11 = f32[32,1,384]{2,1,0:T(1,128)S(1)} all-to-all(f32[32,1,384]{2,1,0:T(1,128)S(1)} %copy.8), channel_id=1, replica_groups=mesh['ccy'=4,'path'=8] {'ccy','path'}, dimensions={0} | all-to-all | bytes 98304 | tf_op jit(solution)/shard_map/all_to_all | solution.py:356
  61.4 0.6 copy.11
  62.0 1.6 %collect.1 = (f32[16,128]{1,0:T(8,128)}, f32[16,64]{1,0:T(8,128)}) custom-call(s32[16]{0:T(128)} %slot_ref.5, f32[32,384]{1,0:T(8,128)} %bitcast.28), custom_call_target="tpu_custom_call" | custom-call | tf_op jit(solution)/shard_map/collect/pallas_call | solution.py:310
Async XLA Ops:
  3.2 10.5 %collective-permute-start.4 = (f32[32,2048]{1,0:T(8,128)S(1)}, f32[32,2048]{1,0:T(8,128)S(1)}, u32[]{:S(2)}, u32[]{:S(2)}) collective-permute-start(f32[32,2048]{1,0:T(8,128)S(1)} %pad_maximum_fusion.flow_ref), channel_id=1, source_target_pairs={{0,16},{8,24},{16,0},{24,8},{1,17},{9,25},{17,1},{25,9},{2,18},{10... | collective-permute-start | bytes 786440 | tf_op jit(solution)/shard_map/ppermute | solution.py:332
  13.6 18.5 %copy-start = (s32[16]{0:T(128)S(1)}, s32[16]{0:T(128)}, u32[]{:S(2)}) copy-start(s32[16]{0:T(128)} %slot_ref.5) | copy-start | bytes 196
  13.6 22.3 %collective-permute-start.3 = (bf16[8,512,128]{2,1,0:T(8,128)(2,1)S(1)}, bf16[8,512,128]{2,1,0:T(8,128)(2,1)S(1)}, u32[]{:S(2)}, u32[]{:S(2)}) collective-permute-start(bf16[8,512,128]{2,1,0:T(8,128)(2,1)S(1)} %shard_map.77.refs_0_), channel_id=1, source_target_pairs={{0,8},{8,0},{16,24},{24,16},{1,9},{9,1},{17,25},{25,17},{2,10},{10... | collective-permute-start | bytes 3145736 | tf_op jit(solution)/shard_map/ppermute | solution.py:332
  21.2 14.7 %collective-permute-start.5 = (bf16[8,512,128]{2,1,0:T(8,128)(2,1)S(1)}, bf16[8,512,128]{2,1,0:T(8,128)(2,1)}, u32[]{:S(2)}, u32[]{:S(2)}) collective-permute-start(bf16[8,512,128]{2,1,0:T(8,128)(2,1)S(1)} %shard_map.78.refs_2_), channel_id=1, source_target_pairs={{0,8},{8,0},{16,24},{24,16},{1,9},{9,1},{17,25},{25,17},{2,10},{10... | collective-permute-start | bytes 3145736 | tf_op jit(solution)/shard_map/ppermute | solution.py:332
  23.6 1.9 %collective-permute-start = (bf16[2,64,512]{2,1,0:T(8,128)(2,1)}, bf16[2,64,512]{2,1,0:T(8,128)(2,1)S(1)}, u32[]{:S(2)}, u32[]{:S(2)}) collective-permute-start(bf16[2,64,512]{2,1,0:T(8,128)(2,1)} %get-tuple-element.11), channel_id=1, source_target_pairs={{0,8},{8,0},{16,24},{24,16},{1,9},{9,1},{17,25},{25,17},{2,10},{10... | collective-permute-start | bytes 393224 | tf_op jit(solution)/shard_map/ppermute | solution.py:332
  23.6 6.6 %collective-permute-start.1 = (bf16[2,64,512]{2,1,0:T(8,128)(2,1)}, bf16[2,64,512]{2,1,0:T(8,128)(2,1)S(1)}, u32[]{:S(2)}, u32[]{:S(2)}) collective-permute-start(bf16[2,64,512]{2,1,0:T(8,128)(2,1)} %get-tuple-element.13), channel_id=1, source_target_pairs={{0,16},{8,24},{16,0},{24,8},{1,17},{9,25},{17,1},{25,9},{2,18},{10... | collective-permute-start | bytes 393224 | tf_op jit(solution)/shard_map/ppermute | solution.py:332
  24.2 7.9 %collective-permute-start.2 = (bf16[2,64,512]{2,1,0:T(8,128)(2,1)}, bf16[2,64,512]{2,1,0:T(8,128)(2,1)}, u32[]{:S(2)}, u32[]{:S(2)}) collective-permute-start(bf16[2,64,512]{2,1,0:T(8,128)(2,1)} %get-tuple-element.10), channel_id=1, source_target_pairs={{0,24},{8,16},{16,8},{24,0},{1,25},{9,17},{17,9},{25,1},{2,26},{10... | collective-permute-start | bytes 393224 | tf_op jit(solution)/shard_map/ppermute | solution.py:332
  35.9 0.8 %copy-start.1 = (f32[16,512]{1,0:T(8,128)S(1)}, f32[16,512]{1,0:T(8,128)}, u32[]{:S(2)}) copy-start(f32[16,512]{1,0:T(8,128)} %weight_ref.1) | copy-start | bytes 98308

commit v3 on v2

--- a/solution.py
+++ b/solution.py
@@ -22,7 +22,6 @@
 NN = (((1,), (0,)), ((), ()))
 TN = (((0,), (0,)), ((), ()))
 VM = pl.BlockSpec(memory_space=pltpu.VMEM)
-SM = pl.BlockSpec(memory_space=pltpu.SMEM)
 
 
 def dot16(a, b, dims):
@@ -127,27 +126,43 @@
         cost_estimate=pl.CostEstimate(
             flops=4 * trades * NSETS * CFG, bytes_accessed=2**21, transcendentals=0
         ),
-        compiler_params=pltpu.CompilerParams(vmem_limit_bytes=16 * 2**20),
+        compiler_params=pltpu.CompilerParams(vmem_limit_bytes=12 * 2**20),
     )(flows)
 
 
-def date_of(slot_ref, station_ref, slots, k):
-    mine = station_ref[0] * slots + k
-    date, found = 0, 0
-    for d in range(slot_ref.shape[0]):
-        hit = slot_ref[d] == mine
-        date = jnp.where(hit, d, date)
-        found = jnp.where(hit, 1, found)
-    return date, found
-
-
-def disc_kernel(groups, slot_ref, station_ref, *refs):
-    curves, (disc_ref, scaled_ref, rhs) = refs[:groups], refs[groups:]
-    slots, nodes, paths = curves[0].shape
-    depth = rhs.shape[0]
-    rhs[3 * nodes :, :] = jnp.ones((depth - 3 * nodes, paths), jnp.bfloat16)
+def prepare_kernel(groups, stations, scale, *refs):
+    sources, outs, scratch = refs[:6], refs[6 : 12 + groups], refs[12 + groups :]
+    flow_ref, left_ref, scaled_ref, column_ref, pick_ref, route_ref, *pieces = outs
+    copies = [
+        pltpu.make_async_copy(source, held, scratch[6].at[i])
+        for i, (source, held) in enumerate(zip(sources, scratch[:6]))
+    ]
+    for copy in copies:
+        copy.start()
+    for copy in copies:
+        copy.wait()
+    index_ref, amount_ref, set_ref, curve_ref, weight_ref, slot_ref = scratch[:6]
+    ncf = index_ref.shape[0]
+    slots, nodes, total_paths = curve_ref.shape
+    paths = total_paths // groups
+    dates = slot_ref.shape[0]
+    station, member = lax.axis_index("path"), lax.axis_index("ccy")
+    code = index_ref[...] + CFG * set_ref[...]
+    flow_ref[:ncf, :] = code.astype(jnp.float32)
+    flow_ref[ncf:, :] = amount_ref[...]
+    for mask, piece in enumerate(pieces):
+        begin = pl.multiple_of((member ^ mask) * paths, LANES)
+        for k in range(slots):
+            piece[k] = curve_ref[k, :, pl.ds(begin, paths)]
+    lead = (lax.broadcasted_iota(jnp.int32, (8, LANES), 0) == 0).astype(jnp.float32)
     for k in range(slots):
-        date, _ = date_of(slot_ref, station_ref, slots, k)
+        date, found = 0, 0
+        for d in range(dates):
+            hit = slot_ref[d] == station * slots + k
+            date = jnp.where(hit, d, date)
+            found = jnp.where(hit, 1, found)
+        row = weight_ref[pl.ds(date, 1), :] * (0.5 * scale) * found.astype(jnp.float32)
+        column_ref[k] = dot_full(jnp.broadcast_to(row, (8, NSETS)), lead, TN)
         start = 0.5 * (date.astype(jnp.float32) + 1.0)
         grid = lax.broadcasted_iota(jnp.int32, (CFG, nodes), 0).astype(jnp.float32)
         remain = HORIZON * (grid + 1.0) / CFG - start
@@ -163,27 +178,78 @@
         low = (rest - mid.astype(jnp.float32)).astype(jnp.bfloat16)
         dead = jnp.where((node == 0.0) & (remain <= 0.0), -1e30, 0.0).astype(jnp.bfloat16)
         left = jnp.concatenate([high, mid, low, dead], axis=1)
+        for i in range(4 * nodes // LANES):
+            left_ref[k, i] = left[:, i * LANES : (i + 1) * LANES]
+    line = lax.broadcasted_iota(jnp.int32, (dates, LANES), 0)
+    slot_of = jnp.zeros((dates, LANES), jnp.int32)
+    for d in range(dates):
+        slot_of = jnp.where(line == d, slot_ref[d], slot_of)
+    for i in range(stations * slots):
+        pick_ref[i] = (slot_of == i).astype(jnp.float32)
+    for g in range(groups):
+        for m in range(groups):
+            chosen = ((member ^ g) == m).astype(jnp.float32)
+            route_ref[g * groups + m] = jnp.full((8, LANES), chosen, jnp.float32)
+
+
+def prepare(date_slot, index, amount, sets, curve, weights, groups, stations):
+    ncf, trades = index.shape
+    slots, nodes, total_paths = curve.shape
+    dates = date_slot.shape[0]
+    sources = (index, amount, sets, curve, weights, date_slot)
+    return pl.pallas_call(
+        functools.partial(prepare_kernel, groups, stations, 1.0 / total_paths),
+        out_shape=(
+            jax.ShapeDtypeStruct((2 * ncf, trades), jnp.float32),
+            jax.ShapeDtypeStruct((slots, 4 * nodes // LANES, CFG, LANES), jnp.bfloat16),
+            jax.ShapeDtypeStruct((slots, CFG, nodes), jnp.float32),
+            jax.ShapeDtypeStruct((slots, NSETS, LANES), jnp.float32),
+            jax.ShapeDtypeStruct((stations * slots, dates, LANES), jnp.float32),
+            jax.ShapeDtypeStruct((groups * groups, 8, LANES), jnp.float32),
+        )
+        + (jax.ShapeDtypeStruct((slots, nodes, total_paths // groups), jnp.bfloat16),) * groups,
+        in_specs=[pl.BlockSpec(memory_space=pltpu.HBM)] * 6,
+        out_specs=(VM,) * (6 + groups),
+        scratch_shapes=[pltpu.VMEM(source.shape, source.dtype) for source in sources[:5]]
+        + [pltpu.SMEM((dates,), jnp.int32), pltpu.SemaphoreType.DMA((6,))],
+        cost_estimate=pl.CostEstimate(flops=2**22, bytes_accessed=2**21, transcendentals=0),
+        compiler_params=pltpu.CompilerParams(
+            vmem_limit_bytes=14 * 2**20 + 6 * slots * nodes * total_paths
+        ),
+        name="prepare",
+    )(*[pltpu.with_memory_space_constraint(source, pltpu.HBM) for source in sources])
+
+
+def grant(own, shared):
+    return own if shared <= 2**24 else 62 * 2**20
+
+
+def disc_kernel(groups, left_ref, *refs):
+    curves, (disc_ref, rhs) = refs[:groups], refs[groups:]
+    slots, nodes, paths = curves[0].shape
+    depth = rhs.shape[0]
+    rhs[3 * nodes :, :] = jnp.ones((depth - 3 * nodes, paths), jnp.bfloat16)
+    for k in range(slots):
+        left = join(left_ref.at[k], range(depth // LANES))
         for g in range(groups):
-            part = curves[g][k]
             for copy in range(3):
-                rhs[copy * nodes : (copy + 1) * nodes, :] = part
+                rhs[copy * nodes : (copy + 1) * nodes, :] = curves[g][k]
             for p0 in range(0, paths, WIDE):
                 block = jnp.exp2(dot16(left, rhs[:, p0 : p0 + WIDE], NN)).astype(jnp.bfloat16)
                 for i in range(WIDE // LANES):
                     disc_ref[k, g, p0 // LANES + i] = block[:, i * LANES : (i + 1) * LANES]
 
 
-def discounts(date_slot, station, curves):
+def discounts(left, curves):
     slots, nodes, paths = curves[0].shape
     groups = len(curves)
     return pl.pallas_call(
         functools.partial(disc_kernel, groups),
-        out_shape=(
-            jax.ShapeDtypeStruct((slots, groups, paths // LANES, CFG, LANES), jnp.bfloat16),
-            jax.ShapeDtypeStruct((slots, CFG, nodes), jnp.float32),
-        ),
-        in_specs=[SM, SM] + [VM] * groups,
-        out_specs=(VM, VM),
+        out_shape=jax.ShapeDtypeStruct(
+            (slots, groups, paths // LANES, CFG, LANES), jnp.bfloat16
+        ),
+        in_specs=[VM] * (1 + groups),
+        out_specs=VM,
         scratch_shapes=[pltpu.VMEM((4 * nodes, paths), jnp.bfloat16)],
         cost_estimate=pl.CostEstimate(
             flops=2 * slots * groups * CFG * paths * 4 * nodes,
@@ -191,14 +257,13 @@
             transcendentals=slots * groups * CFG * paths,
         ),
         compiler_params=pltpu.CompilerParams(
-            vmem_limit_bytes=8 * 2**20 + 3 * slots * groups * CFG * paths
+            vmem_limit_bytes=grant(6 * 2**20, 2 * slots * groups * CFG * paths)
         ),
         name="discounts",
-    )(date_slot, station, *curves)
-
-
-def price_kernel(stations, scale, slot_ref, station_ref, member_ref, weight_ref, scaled_ref,
-                 disc_ref, *refs):
+    )(left, *curves)
+
+
+def price_kernel(stations, scale, column_ref, scaled_ref, route_ref, disc_ref, *refs):
     groups = disc_ref.shape[1]
     tables = refs[:groups]
     out_ref, slope_ref, expo_ref, pull_ref, sens_ref = refs[groups:]
@@ -208,12 +273,9 @@
     nodes = scaled_ref.shape[2]
     share = NSETS // groups
     wide = WIDE // LANES
-    lead = (lax.broadcasted_iota(jnp.int32, (8, LANES), 0) == 0).astype(jnp.float32)
     pull_ref[...] = jnp.zeros_like(pull_ref)
     for k in range(slots):
-        date, found = date_of(slot_ref, station_ref, slots, k)
-        row = weight_ref[pl.ds(date, 1), :] * (0.5 * scale) * found.astype(jnp.float32)
-        column = dot_full(jnp.broadcast_to(row, (8, NSETS)), lead, TN)
+        column = column_ref[k]
         folded = jnp.zeros((NSETS, LANES), jnp.float32)
         left = jnp.concatenate([join(tables[g], range(cblocks)) for g in range(groups)], axis=1)
         for p0 in range(0, pblocks, wide):
@@ -246,15 +308,19 @@
         sens_ref[k] = dot_full(pull_ref[...], scaled_ref[k], NN)
     for g in range(groups):
         rows = slice(g * stations, (g + 1) * stations)
-        mask = member_ref[0] ^ g
         for k in range(slots):
             part = expo_ref[k : k + 1, g * share : (g + 1) * share]
-            out_ref[rows, k * share : (k + 1) * share] = jnp.broadcast_to(part, (stations, share))
-        line = jnp.concatenate([sens_ref[k, pl.ds(mask, 1), :] for k in range(slots)], axis=1)
-        out_ref[rows, slots * share :] = jnp.broadcast_to(line, (stations, slots * nodes))
-
-
-def price(date_slot, station, member, weights, scaled, disc, tables, stations, total_paths):
+            out_ref[rows, 0, k * share : (k + 1) * share] = jnp.broadcast_to(
+                part, (stations, share)
+            )
+            line = jnp.zeros((1, nodes), jnp.float32)
+            for m in range(groups):
+                line = line + route_ref[g * groups + m, 0:1, :nodes] * sens_ref[k, m : m + 1, :]
+            begin = slots * share + k * nodes
+            out_ref[rows, 0, begin : begin + nodes] = jnp.broadcast_to(line, (stations, nodes))
+
+
+def price(column, scaled, route, disc, tables, stations, total_paths):
     slots, groups, pblocks = disc.shape[:3]
     nodes = scaled.shape[2]
     paths = pblocks * LANES
@@ -262,9 +328,9 @@
     return pl.pallas_call(
         functools.partial(price_kernel, stations, 1.0 / total_paths),
         out_shape=jax.ShapeDtypeStruct(
-            (groups * stations, slots * (NSETS // groups + nodes)), jnp.float32
-        ),
-        in_specs=[SM] * 3 + [VM] * (3 + groups),
+            (groups * stations, 1, slots * (NSETS // groups + nodes)), jnp.float32
+        ),
+        in_specs=[VM] * (4 + groups),
         out_specs=VM,
         scratch_shapes=[
             pltpu.VMEM((pblocks, NSETS, LANES), jnp.bfloat16),
@@ -278,68 +344,60 @@
             transcendentals=slots * NSETS * paths,
         ),
         compiler_params=pltpu.CompilerParams(
-            vmem_limit_bytes=16 * 2**20 + 3 * slots * groups * CFG * paths // 2
+            vmem_limit_bytes=grant(10 * 2**20, 2 * slots * groups * CFG * paths)
         ),
         name="price",
-    )(date_slot, station, member, weights, scaled, disc, *tables)
-
-
-def collect_kernel(groups, slots, nodes, slot_ref, got_ref, expo_ref, sens_ref, sum_ref):
-    stations = sum_ref.shape[0]
+    )(column, scaled, route, disc, *tables)
+
+
+def collect_kernel(groups, slots, nodes, pick_ref, got_ref, expo_ref, sens_ref):
+    stations = got_ref.shape[0] // groups
     dates, share = expo_ref.shape
-    total = got_ref[:stations]
-    for g in range(1, groups):
-        total = total + got_ref[g * stations : (g + 1) * stations]
-    sum_ref[...] = total
-    for d in range(dates):
-        slot = slot_ref[d]
-        line = sum_ref[pl.ds(slot // slots, 1), :]
-        expo, sens = line[:, :share], line[:, slots * share : slots * share + nodes]
-        for k in range(1, slots):
-            here = slot % slots == k
+    expo = jnp.zeros((dates, share), jnp.float32)
+    sens = jnp.zeros((dates, nodes), jnp.float32)
+    for p in range(stations):
+        line = got_ref[p]
+        for g in range(1, groups):
+            line = line + got_ref[g * stations + p]
+        for k in range(slots):
+            pick = pick_ref[p * slots + k]
             begin = slots * share + k * nodes
-            expo = jnp.where(here, line[:, k * share : (k + 1) * share], expo)
-            sens = jnp.where(here, line[:, begin : begin + nodes], sens)
-        expo_ref[d : d + 1, :] = expo
-        sens_ref[d : d + 1, :] = sens
-
-
-def collect(date_slot, got, groups, slots, nodes):
-    dates = date_slot.shape[0]
-    share = NSETS // groups
+            mine = pick[:, :share] if share <= LANES else pick[:, :1]
+            expo = expo + mine * line[:, k * share : (k + 1) * share]
+            sens = sens + pick[:, :nodes] * line[:, begin : begin + nodes]
+    expo_ref[...] = expo
+    sens_ref[...] = sens
+
+
+def collect(pick, got, groups, slots, nodes):
+    dates = pick.shape[1]
     return pl.pallas_call(
         functools.partial(collect_kernel, groups, slots, nodes),
         out_shape=(
-            jax.ShapeDtypeStruct((dates, share), jnp.float32),
+            jax.ShapeDtypeStruct((dates, NSETS // groups), jnp.float32),
             jax.ShapeDtypeStruct((dates, nodes), jnp.float32),
         ),
-        in_specs=[SM, VM],
+        in_specs=[VM, VM],
         out_specs=(VM, VM),
-        scratch_shapes=[pltpu.VMEM((got.shape[0] // groups, got.shape[1]), jnp.float32)],
+        compiler_params=pltpu.CompilerParams(vmem_limit_bytes=6 * 2**20),
         name="collect",
-    )(date_slot, got)
+    )(pick, got)
 
 
 def local(curve_store, cash_index, cash_amount, trade_set, date_slot, default_weight):
     groups = lax.axis_size("ccy")
     stations = lax.axis_size("path")
-    member = lax.axis_index("ccy").astype(jnp.int32)
-    station = lax.axis_index("path").astype(jnp.int32)
     _, slots, nodes, total_paths = curve_store.shape
-    paths = total_paths // groups
 
     def swap(array, mask):
         return lax.ppermute(array, "ccy", [(i, i ^ mask) for i in range(groups)])
 
-    code = jnp.swapaxes(cash_index[0], 0, 1) + CFG * trade_set
-    flows = jnp.concatenate([code.astype(jnp.float32), jnp.swapaxes(cash_amount[0], 0, 1)], axis=0)
+    flows, left, scaled, column, pick, route, *pieces = prepare(
+        date_slot, jnp.swapaxes(cash_index[0], 0, 1), jnp.swapaxes(cash_amount[0], 0, 1),
+        trade_set, curve_store[0], default_weight, groups, stations,
+    )
     others = {m: swap(flows, m) for m in range(2, groups, 2)}
-
-    def piece(mask):
-        begin = (member ^ mask) * paths
-        return lax.dynamic_slice_in_dim(curve_store[0], begin, paths, 2)
-
-    curves = [piece(0)] + [swap(piece(m), m) for m in range(1, groups)]
+    curves = [pieces[0]] + [swap(pieces[m], m) for m in range(1, groups)]
 
     tables = {0: build_table(flows)}
     for m in others:
@@ -348,13 +406,10 @@
         tables[m + 1] = swap(tables[m], 1)
     tables = [tables[m] for m in range(groups)]
 
-    disc, scaled = discounts(date_slot, station[None], curves)
-    payload = price(
-        date_slot, station[None], member[None], default_weight, scaled, disc, tables,
-        stations, total_paths,
-    )
+    disc = discounts(left, curves)
+    payload = price(column, scaled, route, disc, tables, stations, total_paths)
     got = lax.all_to_all(payload, ("ccy", "path"), 0, 0, tiled=True)
-    expo, sens = collect(date_slot, got, groups, slots, nodes)
+    expo, sens = collect(pick, got, groups, slots, nodes)
     return expo, sens[None]
 
 

time: 64 us -> 55.7 us (0.87)
  local copies, waits for them, and re-layouts: 3.3 us -> 0 us
  other arithmetic: 2.57 us -> 0 us
  Pallas kernels: 32.9 us -> 31.1 us
    pallas_call x1, Pallas kernels: 12.8 us -> 10.7 us  [price(): pl.pallas_call(functools.partial(price_kernel, stations, 1.0 / total_path...]
    dynamic_slice x1 -> x0, local copies, waits for them, and re-layouts: 1.85 us -> none  [piece(): return lax.dynamic_slice_in_dim(curve_store[0], begin, paths, 2)]
    unnamed x5 -> x0, local copies, waits for them, and re-layouts: 1.38 us -> none
    pallas_call x1 -> x2, Pallas kernels: 3.72 us -> 4.85 us  [the longest x1 2.52 us: prepare(): pl.pallas_call(functools.partial(prepare_kernel, groups, stations, 1.0 /...]
    concatenate x1 -> x0, other arithmetic: 0.94 us -> none  [local(): jnp.concatenate([code.astype(jnp.float32), jnp.swapaxes(cash_amount[0], 0...]
    convert_element_type x1 -> x0, other arithmetic: 0.92 us -> none  [local(): code.astype(jnp.float32)]
    pallas_call x1, Pallas kernels: 1.58 us -> 0.69 us  [collect(): pl.pallas_call(functools.partial(collect_kernel, groups, slots, nodes), o...]
    mul x1 -> x0, other arithmetic: 0.71 us -> none  [local(): code = jnp.swapaxes(cash_index[0], 0, 1) + CFG * trade_set]
  transfers between devices with their start and end apart: 6 -> 6, of which waited for: 2 -> 3; matrix products, arithmetic and copies ran while one was open for 3% -> 0% of each run, Pallas kernels for 29% -> 31%
where the time goes in v3:
time: 55.7 us; the launch traced here: 55.6 us
  Pallas kernels  31.1 us (56%)
  blocking collectives  12 us (22%)
  waiting for transfers between devices  6.32 us (11%)
  starting transfers between devices  5.5 us (10%)
  between operations  0.71 us (1%)
    pallas_call x2, Pallas kernels, build_table(): pl.pallas_call(table_kernel, out_shape=jax.ShapeDtypeStruct((CFG // LANES...  14.8 us
    all_to_all x1, blocking collectives, local(): got = lax.all_to_all(payload, ('ccy', 'path'), 0, 0, tiled=True)  12 us
    pallas_call x1, Pallas kernels, price(): pl.pallas_call(functools.partial(price_kernel, stations, 1.0 / total_path...  10.7 us
    ppermute x6, waiting for transfers between devices, swap(): return lax.ppermute(array, 'ccy', [(i, i ^ mask) for i in range(groups)])  6.32 us
    ppermute x6, starting transfers between devices, swap(): return lax.ppermute(array, 'ccy', [(i, i ^ mask) for i in range(groups)])  5.5 us
    pallas_call x1, Pallas kernels, prepare(): pl.pallas_call(functools.partial(prepare_kernel, groups, stations, 1.0 /...  2.52 us
    pallas_call x1, Pallas kernels, discounts(): pl.pallas_call(functools.partial(disc_kernel, groups), out_shape=jax.Shap...  2.33 us
  transfers between devices with their start and end apart: 6, of which 3 were waited for; matrix products, arithmetic and copies ran while one was open for 0% of the time, Pallas kernels for 31%

profile of v3, /device:TPU:0, one launch (start us, length us, event | category | flops | bytes accessed | tf_op | source)
XLA Modules:
  0.0 55.6 jit_solution(3504036783408192686)
XLA Ops:
  0.6 2.5 %prepare.1 = (f32[32,2048]{1,0:T(8,128)S(1)}, bf16[2,2,1024,128]{3,2,1,0:T(8,128)(2,1)S(1)}, f32[2,1024,64]{2,1,0:T(8,128)S(1)}, f32[2,512,128]{2,1,0:T(8,128)S(...) custom-call(s32[16,2048]{1,0:T(8,128)} %bitcast.9, ...), custom_call_target="tpu_custom_call" | custom-call | flops 4194304 | bytes 2097152 | tf_op jit(solution)/shard_map/prepare/pallas_call | solution.py:200
  3.2 3.0 %collective-permute-start.4 = (f32[32,2048]{1,0:T(8,128)S(1)}, f32[32,2048]{1,0:T(8,128)S(1)}, u32[]{:S(2)}, u32[]{:S(2)}) collective-permute-start(f32[32,2048]{1,0:T(8,128)S(1)} %get-tuple-element.23.flow_ref), channel_id=1, source_target_pairs={{0,16},{8,24},{16,0},{24,8},{1,17},{9,25},{17,1},{25,9},{2,18},{10... | collective-permute-start | bytes 786440 | tf_op jit(solution)/shard_map/ppermute | solution.py:393
  6.2 7.3 %shard_map.77.refs_0_ = bf16[8,512,128]{2,1,0:T(8,128)(2,1)S(1)} custom-call(f32[32,2048]{1,0:T(8,128)S(1)} %get-tuple-element.23.flow_ref), custom_call_target="tpu_custom_call" | custom-call | flops 4294967296 | bytes 2097152 | tf_op jit(solution)/shard_map/pallas_call | solution.py:113
  13.5 0.1 collective-permute-start.3
  13.6 0.0 collective-permute-done.4.flow_ref
  13.6 7.5 %shard_map.78.refs_2_ = bf16[8,512,128]{2,1,0:T(8,128)(2,1)S(1)} custom-call(f32[32,2048]{1,0:T(8,128)S(1)} %collective-permute-done.4.flow_ref), custom_call_target="tpu_custom_call" | custom-call | flops 4294967296 | bytes 2097152 | tf_op jit(solution)/shard_map/pallas_call | solution.py:113
  21.1 0.5 collective-permute-start.5
  21.7 0.1 collective-permute-start
  21.7 0.6 %collective-permute-start.1 = (bf16[2,64,512]{2,1,0:T(8,128)(2,1)S(1)}, bf16[2,64,512]{2,1,0:T(8,128)(2,1)S(1)}, u32[]{:S(2)}, u32[]{:S(2)}) collective-permute-start(bf16[2,64,512]{2,1,0:T(8,128)(2,1)S(1)} %get-tuple-element.21), channel_id=1, source_target_pairs={{0,16},{8,24},{16,0},{24,8},{1,17},{9,25},{17,1},{25,9},{2,18},{10... | collective-permute-start | bytes 393224 | tf_op jit(solution)/shard_map/ppermute | solution.py:393
  22.3 1.2 %collective-permute-start.2 = (bf16[2,64,512]{2,1,0:T(8,128)(2,1)S(1)}, bf16[2,64,512]{2,1,0:T(8,128)(2,1)S(1)}, u32[]{:S(2)}, u32[]{:S(2)}) collective-permute-start(bf16[2,64,512]{2,1,0:T(8,128)(2,1)S(1)} %get-tuple-element.22), channel_id=1, source_target_pairs={{0,24},{8,16},{16,8},{24,0},{1,25},{9,17},{17,9},{25,1},{2,26},{10... | collective-permute-start | bytes 393224 | tf_op jit(solution)/shard_map/ppermute | solution.py:393
  23.5 0.6 %collective-permute-done.refs_1_ = bf16[2,64,512]{2,1,0:T(8,128)(2,1)S(1)} collective-permute-done((bf16[2,64,512]{2,1,0:T(8,128)(2,1)S(1)}, bf16[2,64,512]{2,1,0:T(8,128)(2,1)S(1)}, u32[]{:S(2)}, u32[]{:S(2)}) %collective-permute-start) | collective-permute-done | bytes 131104 | tf_op jit(solution)/shard_map/ppermute | solution.py:393
  24.1 4.0 %collective-permute-done.1.refs_2_ = bf16[2,64,512]{2,1,0:T(8,128)(2,1)S(1)} collective-permute-done((bf16[2,64,512]{2,1,0:T(8,128)(2,1)S(1)}, bf16[2,64,512]{2,1,0:T(8,128)(2,1)S(1)}, u32[]{:S(2)}, u32[]{:S(2)}) %collective-permute-start.1) | collective-permute-done | bytes 131104 | tf_op jit(solution)/shard_map/ppermute | solution.py:393
  28.1 1.7 %collective-permute-done.2.refs_3_ = bf16[2,64,512]{2,1,0:T(8,128)(2,1)S(1)} collective-permute-done((bf16[2,64,512]{2,1,0:T(8,128)(2,1)S(1)}, bf16[2,64,512]{2,1,0:T(8,128)(2,1)S(1)}, u32[]{:S(2)}, u32[]{:S(2)}) %collective-permute-start.2) | collective-permute-done | bytes 131104 | tf_op jit(solution)/shard_map/ppermute | solution.py:393
  29.8 2.3 %discounts.1.disc_ref = bf16[2,4,4,1024,128]{4,3,2,1,0:T(8,128)(2,1)S(1)} custom-call(bf16[2,2,1024,128]{3,2,1,0:T(8,128)(2,1)S(1)} %get-tuple-element.18.left_ref, bf16[2,64,512]{2,1,0:T(8,128)(2,1)S(1)} %get-tuple-element.19.refs_0_, bf16[2,64,512]{2,1,0:T(8,128)(2,1)S(1)} %collective-permute-done.refs_1_, ...), custom_call_target="tpu_custom_call" | custom-call | flops 2147483648 | bytes 8388608 | tf_op jit(solution)/shard_map/discounts/pallas_call | solution.py:246
  32.2 0.0 collective-permute-done.3.refs_1_
  32.2 0.0 collective-permute-done.5.refs_3_
  32.2 10.7 %price.1 = f32[32,1,384]{2,1,0:T(1,128)S(1)} custom-call(f32[2,512,128]{2,1,0:T(8,128)S(1)} %get-tuple-element.15.column_ref, f32[2,1024,64]{2,1,0:T(8,128)S(1)} %get-tuple-element.16.scaled_ref, f32[16,8,128]{2,1,0:T(8,128)S(1)} %get-tuple-element.17.route_ref, bf16[2,4,4,1024,128]{4,3,2,1,0:T(8,128)(2,1)S(1)} %discounts.1.disc_ref, ...), custom_call_target="tpu_custom_call" | custom-call | flops 8589934592 | bytes 8388608 | tf_op jit(solution)/shard_map/price/pallas_call | solution.py:328
  42.9 12.0 %all_to_all.5.got_ref = f32[32,1,384]{2,1,0:T(1,128)S(1)} all-to-all(f32[32,1,384]{2,1,0:T(1,128)S(1)} %price.1), channel_id=1, replica_groups=mesh['ccy'=4,'path'=8] {'ccy','path'}, dimensions={0} | all-to-all | bytes 98304 | tf_op jit(solution)/shard_map/all_to_all | solution.py:411
  54.9 0.7 %collect.1 = (f32[16,128]{1,0:T(8,128)}, f32[16,64]{1,0:T(8,128)}) custom-call(f32[16,16,128]{2,1,0:T(8,128)S(1)} %get-tuple-element.14.pick_ref, f32[32,1,384]{2,1,0:T(1,128)S(1)} %all_to_all.5.got_ref), custom_call_target="tpu_custom_call" | custom-call | tf_op jit(solution)/shard_map/collect/pallas_call | solution.py:374
Async XLA Ops:
  3.2 10.4 %collective-permute-start.4 = (f32[32,2048]{1,0:T(8,128)S(1)}, f32[32,2048]{1,0:T(8,128)S(1)}, u32[]{:S(2)}, u32[]{:S(2)}) collective-permute-start(f32[32,2048]{1,0:T(8,128)S(1)} %get-tuple-element.23.flow_ref), channel_id=1, source_target_pairs={{0,16},{8,24},{16,0},{24,8},{1,17},{9,25},{17,1},{25,9},{2,18},{10... | collective-permute-start | bytes 786440 | tf_op jit(solution)/shard_map/ppermute | solution.py:393
  13.5 18.7 %collective-permute-start.3 = (bf16[8,512,128]{2,1,0:T(8,128)(2,1)S(1)}, bf16[8,512,128]{2,1,0:T(8,128)(2,1)S(1)}, u32[]{:S(2)}, u32[]{:S(2)}) collective-permute-start(bf16[8,512,128]{2,1,0:T(8,128)(2,1)S(1)} %shard_map.77.refs_0_), channel_id=1, source_target_pairs={{0,8},{8,0},{16,24},{24,16},{1,9},{9,1},{17,25},{25,17},{2,10},{10... | collective-permute-start | bytes 3145736 | tf_op jit(solution)/shard_map/ppermute | solution.py:393
  21.1 11.1 %collective-permute-start.5 = (bf16[8,512,128]{2,1,0:T(8,128)(2,1)S(1)}, bf16[8,512,128]{2,1,0:T(8,128)(2,1)S(1)}, u32[]{:S(2)}, u32[]{:S(2)}) collective-permute-start(bf16[8,512,128]{2,1,0:T(8,128)(2,1)S(1)} %shard_map.78.refs_2_), channel_id=1, source_target_pairs={{0,8},{8,0},{16,24},{24,16},{1,9},{9,1},{17,25},{25,17},{2,10},{10... | collective-permute-start | bytes 3145736 | tf_op jit(solution)/shard_map/ppermute | solution.py:393
  21.7 2.5 %collective-permute-start = (bf16[2,64,512]{2,1,0:T(8,128)(2,1)S(1)}, bf16[2,64,512]{2,1,0:T(8,128)(2,1)S(1)}, u32[]{:S(2)}, u32[]{:S(2)}) collective-permute-start(bf16[2,64,512]{2,1,0:T(8,128)(2,1)S(1)} %get-tuple-element.20), channel_id=1, source_target_pairs={{0,8},{8,0},{16,24},{24,16},{1,9},{9,1},{17,25},{25,17},{2,10},{10... | collective-permute-start | bytes 393224 | tf_op jit(solution)/shard_map/ppermute | solution.py:393
  21.7 6.4 %collective-permute-start.1 = (bf16[2,64,512]{2,1,0:T(8,128)(2,1)S(1)}, bf16[2,64,512]{2,1,0:T(8,128)(2,1)S(1)}, u32[]{:S(2)}, u32[]{:S(2)}) collective-permute-start(bf16[2,64,512]{2,1,0:T(8,128)(2,1)S(1)} %get-tuple-element.21), channel_id=1, source_target_pairs={{0,16},{8,24},{16,0},{24,8},{1,17},{9,25},{17,1},{25,9},{2,18},{10... | collective-permute-start | bytes 393224 | tf_op jit(solution)/shard_map/ppermute | solution.py:393
  22.3 7.5 %collective-permute-start.2 = (bf16[2,64,512]{2,1,0:T(8,128)(2,1)S(1)}, bf16[2,64,512]{2,1,0:T(8,128)(2,1)S(1)}, u32[]{:S(2)}, u32[]{:S(2)}) collective-permute-start(bf16[2,64,512]{2,1,0:T(8,128)(2,1)S(1)} %get-tuple-element.22), channel_id=1, source_target_pairs={{0,24},{8,16},{16,8},{24,0},{1,25},{9,17},{17,9},{25,1},{2,26},{10... | collective-permute-start | bytes 393224 | tf_op jit(solution)/shard_map/ppermute | solution.py:393

commit v4 on v3

--- a/solution.py
+++ b/solution.py
@@ -51,13 +51,9 @@
     def prepare(b, carry):
         cols = pl.ds(pl.multiple_of(b * LANES, LANES), LANES)
         code = flow_ref[:ncf, cols].astype(jnp.int32)
-        amount = flow_ref[ncf:, cols]
+        total = flow_ref[ncf:, cols]
         date = code & (CFG - 1)
         sets = lax.shift_right_logical(code[0:1, :], CFG.bit_length() - 1)
-        total = jnp.zeros((ncf, LANES), jnp.float32)
-        for k in range(ncf):
-            same = date == date[k : k + 1, :]
-            total = total + jnp.where(same, amount[k : k + 1, :], 0.0)
         for k in range(ncf):
             rows = slice(k * SUB, (k + 1) * SUB)
             date_t[b, rows, :] = spread(date[k : k + 1, :]).astype(jnp.int16)
@@ -131,8 +127,8 @@
 
 
 def prepare_kernel(groups, stations, scale, *refs):
-    sources, outs, scratch = refs[:6], refs[6 : 12 + groups], refs[12 + groups :]
-    flow_ref, left_ref, scaled_ref, column_ref, pick_ref, route_ref, *pieces = outs
+    sources, outs, scratch = refs[:6], refs[6 : 11 + groups], refs[11 + groups :]
+    flow_ref, left_ref, column_ref, pick_ref, route_ref, *pieces = outs
     copies = [
         pltpu.make_async_copy(source, held, scratch[6].at[i])
         for i, (source, held) in enumerate(zip(sources, scratch[:6]))
@@ -147,14 +143,19 @@
     paths = total_paths // groups
     dates = slot_ref.shape[0]
     station, member = lax.axis_index("path"), lax.axis_index("ccy")
-    code = index_ref[...] + CFG * set_ref[...]
-    flow_ref[:ncf, :] = code.astype(jnp.float32)
-    flow_ref[ncf:, :] = amount_ref[...]
+    date = index_ref[...]
+    flow_ref[:ncf, :] = (date + CFG * set_ref[...]).astype(jnp.float32)
+    total = jnp.zeros(date.shape, jnp.float32)
+    for k in range(ncf):
+        same = date == index_ref[k : k + 1, :]
+        total = total + jnp.where(same, amount_ref[k : k + 1, :], 0.0)
+    flow_ref[ncf:, :] = total
     for mask, piece in enumerate(pieces):
         begin = pl.multiple_of((member ^ mask) * paths, LANES)
         for k in range(slots):
             piece[k] = curve_ref[k, :, pl.ds(begin, paths)]
     lead = (lax.broadcasted_iota(jnp.int32, (8, LANES), 0) == 0).astype(jnp.float32)
+    starts = []
     for k in range(slots):
         date, found = 0, 0
         for d in range(dates):
@@ -163,21 +164,26 @@
             found = jnp.where(hit, 1, found)
         row = weight_ref[pl.ds(date, 1), :] * (0.5 * scale) * found.astype(jnp.float32)
         column_ref[k] = dot_full(jnp.broadcast_to(row, (8, NSETS)), lead, TN)
-        start = 0.5 * (date.astype(jnp.float32) + 1.0)
-        grid = lax.broadcasted_iota(jnp.int32, (CFG, nodes), 0).astype(jnp.float32)
-        remain = HORIZON * (grid + 1.0) / CFG - start
-        node = lax.broadcasted_iota(jnp.int32, (CFG, nodes), 1).astype(jnp.float32)
-        tenor = HORIZON * (node + 1.0) / nodes
-        clipped = jnp.clip(remain, HORIZON / nodes, HORIZON)
-        weight = jnp.maximum(0.0, 1.0 - jnp.abs(clipped - tenor) * (nodes / HORIZON))
-        scaled = weight * (remain * (-LOG2E))
-        scaled_ref[k] = weight * -remain
-        high = scaled.astype(jnp.bfloat16)
-        rest = scaled - high.astype(jnp.float32)
-        mid = rest.astype(jnp.bfloat16)
-        low = (rest - mid.astype(jnp.float32)).astype(jnp.bfloat16)
-        dead = jnp.where((node == 0.0) & (remain <= 0.0), -1e30, 0.0).astype(jnp.bfloat16)
-        left = jnp.concatenate([high, mid, low, dead], axis=1)
+        starts.append(0.5 * (date.astype(jnp.float32) + 1.0))
+    lane = lax.broadcasted_iota(jnp.int32, (CFG, slots * nodes), 1)
+    start = jnp.zeros((CFG, slots * nodes), jnp.float32)
+    for k in range(slots):
+        start = jnp.where(lane >= k * nodes, starts[k], start)
+    grid = lax.broadcasted_iota(jnp.int32, (CFG, slots * nodes), 0).astype(jnp.float32)
+    remain = HORIZON * (grid + 1.0) / CFG - start
+    node = (lane & (nodes - 1)).astype(jnp.float32)
+    tenor = HORIZON * (node + 1.0) / nodes
+    clipped = jnp.clip(remain, HORIZON / nodes, HORIZON)
+    weight = jnp.maximum(0.0, 1.0 - jnp.abs(clipped - tenor) * (nodes / HORIZON))
+    scaled = weight * (remain * (-LOG2E))
+    high = scaled.astype(jnp.bfloat16)
+    rest = scaled - high.astype(jnp.float32)
+    mid = rest.astype(jnp.bfloat16)
+    low = (rest - mid.astype(jnp.float32)).astype(jnp.bfloat16)
+    dead = jnp.where((node == 0.0) & (remain <= 0.0), -1e30, 0.0).astype(jnp.bfloat16)
+    for k in range(slots):
+        own = slice(k * nodes, (k + 1) * nodes)
+        left = jnp.concatenate([part[:, own] for part in (high, mid, low, dead)], axis=1)
         for i in range(4 * nodes // LANES):
             left_ref[k, i] = left[:, i * LANES : (i + 1) * LANES]
     line = lax.broadcasted_iota(jnp.int32, (dates, LANES), 0)
@@ -202,14 +208,13 @@
         out_shape=(
             jax.ShapeDtypeStruct((2 * ncf, trades), jnp.float32),
             jax.ShapeDtypeStruct((slots, 4 * nodes // LANES, CFG, LANES), jnp.bfloat16),
-            jax.ShapeDtypeStruct((slots, CFG, nodes), jnp.float32),
             jax.ShapeDtypeStruct((slots, NSETS, LANES), jnp.float32),
             jax.ShapeDtypeStruct((stations * slots, dates, LANES), jnp.float32),
             jax.ShapeDtypeStruct((groups * groups, 8, LANES), jnp.float32),
         )
         + (jax.ShapeDtypeStruct((slots, nodes, total_paths // groups), jnp.bfloat16),) * groups,
         in_specs=[pl.BlockSpec(memory_space=pltpu.HBM)] * 6,
-        out_specs=(VM,) * (6 + groups),
+        out_specs=(VM,) * (5 + groups),
         scratch_shapes=[pltpu.VMEM(source.shape, source.dtype) for source in sources[:5]]
         + [pltpu.SMEM((dates,), jnp.int32), pltpu.SemaphoreType.DMA((6,))],
         cost_estimate=pl.CostEstimate(flops=2**22, bytes_accessed=2**21, transcendentals=0),
@@ -263,49 +268,85 @@
     )(left, *curves)
 
 
-def price_kernel(stations, scale, column_ref, scaled_ref, route_ref, disc_ref, *refs):
+def price_kernel(stations, scale, column_ref, left_ref, route_ref, disc_ref, *refs):
     groups = disc_ref.shape[1]
     tables = refs[:groups]
-    out_ref, slope_ref, expo_ref, pull_ref, sens_ref = refs[groups:]
+    out_ref, value_ref, slope_ref, expo_ref, pull_ref, sens_ref = refs[groups:]
     slots = disc_ref.shape[0]
     pblocks = disc_ref.shape[2]
     cblocks = CFG // LANES
-    nodes = scaled_ref.shape[2]
+    nodes = sens_ref.shape[2]
     share = NSETS // groups
     wide = WIDE // LANES
     pull_ref[...] = jnp.zeros_like(pull_ref)
-    for k in range(slots):
+
+    def values(k, p0):
+        left = jnp.concatenate([join(tables[g], range(cblocks)) for g in range(groups)], axis=1)
+        right = jnp.concatenate(
+            [join(disc_ref.at[k, g], range(p0, p0 + wide)) for g in range(groups)], axis=0
+        )
+        value = dot16(left, right, NN)
+        for i in range(wide):
+            value_ref[k, p0 + i] = value[:, i * LANES : (i + 1) * LANES]
+
+    def slopes(k):
         column = column_ref[k]
         folded = jnp.zeros((NSETS, LANES), jnp.float32)
-        left = jnp.concatenate([join(tables[g], range(cblocks)) for g in range(groups)], axis=1)
-        for p0 in range(0, pblocks, wide):
-            right = jnp.concatenate(
-                [join(disc_ref.at[k, g], range(p0, p0 + wide)) for g in range(groups)], axis=0
-            )
-            value = dot16(left, right, NN)
-            for i in range(wide):
-                part = value[:, i * LANES : (i + 1) * LANES]
-                square = part * part + SOFTEN
-                inverse = lax.rsqrt(square)
-                folded = folded + (part + square * inverse)
-                slope = column + column * (part * inverse)
-                slope_ref[p0 + i] = slope.astype(jnp.bfloat16)
+        for p in range(pblocks):
+            part = value_ref[k, p]
+            square = part * part + SOFTEN
+            inverse = lax.rsqrt(square)
+            folded = folded + (part + square * inverse)
+            slope = column + column * (part * inverse)
+            slope_ref[k, p] = slope.astype(jnp.bfloat16)
         summed = dot_full(jnp.ones((8, LANES), jnp.float32), folded, NT)
         expo_ref[k : k + 1, :] = summed[0:1] * (0.5 * scale)
-        slope_all = join(slope_ref, range(pblocks))
+
+    def pulls(k, g):
+        slope_all = join(slope_ref.at[k], range(pblocks))
+        for c0 in range(0, cblocks, wide):
+            right = jnp.concatenate(
+                [disc_ref[k, g, p, c0 * LANES : (c0 + wide) * LANES, :] for p in range(pblocks)],
+                axis=1,
+            )
+            back = dot16(slope_all, right, NT)
+            for i in range(wide):
+                cash = tables[g][c0 + i].astype(jnp.float32)
+                pull = jnp.sum(back[:, i * LANES : (i + 1) * LANES] * cash, axis=0)
+                cols = slice((c0 + i) * LANES, (c0 + i + 1) * LANES)
+                pull_ref[k, g : g + 1, cols] = pull[None]
+
+    for p0 in range(0, pblocks, wide):
+        values(0, p0)
+    for k in range(slots):
+        beside = []
+        if k + 1 < slots:
+            beside = [functools.partial(values, k + 1, p0) for p0 in range(0, pblocks, wide)]
+        elif k > 0:
+            beside = [functools.partial(pulls, k - 1, g) for g in range(groups)]
+        for work in beside[:1]:
+            work()
+        slopes(k)
+        for work in beside[1:]:
+            work()
+    for k in [*range(slots - 2), slots - 1]:
         for g in range(groups):
-            for c0 in range(0, cblocks, wide):
-                right = jnp.concatenate(
-                    [disc_ref[k, g, p, c0 * LANES : (c0 + wide) * LANES, :] for p in range(pblocks)],
-                    axis=1,
-                )
-                back = dot16(slope_all, right, NT)
-                for i in range(wide):
-                    cash = tables[g][c0 + i].astype(jnp.float32)
-                    pull = jnp.sum(back[:, i * LANES : (i + 1) * LANES] * cash, axis=0)
-                    cols = slice((c0 + i) * LANES, (c0 + i + 1) * LANES)
-                    pull_ref[g : g + 1, cols] = pull[None]
-        sens_ref[k] = dot_full(pull_ref[...], scaled_ref[k], NN)
+            pulls(k, g)
+    for k in range(slots):
+        pull = pull_ref[k]
+        terms = []
+        for _ in range(3):
+            term = pull.astype(jnp.bfloat16)
+            pull = pull - term.astype(jnp.float32)
+            terms.append(term.astype(jnp.float32))
+        rows = jnp.concatenate(terms, axis=0).astype(jnp.bfloat16)
+        crossed = dot16(rows, join(left_ref.at[k], range(left_ref.shape[1])), NN)
+        count = pull_ref.shape[1]
+        sens = jnp.zeros((count, nodes), jnp.float32)
+        for i in range(3):
+            for j in range(3):
+                sens = sens + crossed[i * count : (i + 1) * count, j * nodes : (j + 1) * nodes]
+        sens_ref[k] = sens * (1.0 / LOG2E)
     for g in range(groups):
         rows = slice(g * stations, (g + 1) * stations)
         for k in range(slots):
@@ -320,9 +361,9 @@
             out_ref[rows, 0, begin : begin + nodes] = jnp.broadcast_to(line, (stations, nodes))
 
 
-def price(column, scaled, route, disc, tables, stations, total_paths):
+def price(column, left, route, disc, tables, stations, total_paths):
     slots, groups, pblocks = disc.shape[:3]
-    nodes = scaled.shape[2]
+    nodes = left.shape[1] * LANES // 4
     paths = pblocks * LANES
     rows = -(-groups // 8) * 8
     return pl.pallas_call(
@@ -333,9 +374,10 @@
         in_specs=[VM] * (4 + groups),
         out_specs=VM,
         scratch_shapes=[
-            pltpu.VMEM((pblocks, NSETS, LANES), jnp.bfloat16),
+            pltpu.VMEM((slots, pblocks, NSETS, LANES), jnp.float32),
+            pltpu.VMEM((slots, pblocks, NSETS, LANES), jnp.bfloat16),
             pltpu.VMEM((slots, NSETS), jnp.float32),
-            pltpu.VMEM((rows, CFG), jnp.float32),
+            pltpu.VMEM((slots, rows, CFG), jnp.float32),
             pltpu.VMEM((slots, rows, nodes), jnp.float32),
         ],
         cost_estimate=pl.CostEstimate(
@@ -347,7 +389,7 @@
             vmem_limit_bytes=grant(10 * 2**20, 2 * slots * groups * CFG * paths)
         ),
         name="price",
-    )(column, scaled, route, disc, *tables)
+    )(column, left, route, disc, *tables)
 
 
 def collect_kernel(groups, slots, nodes, pick_ref, got_ref, expo_ref, sens_ref):
@@ -392,7 +434,7 @@
     def swap(array, mask):
         return lax.ppermute(array, "ccy", [(i, i ^ mask) for i in range(groups)])
 
-    flows, left, scaled, column, pick, route, *pieces = prepare(
+    flows, left, column, pick, route, *pieces = prepare(
         date_slot, jnp.swapaxes(cash_index[0], 0, 1), jnp.swapaxes(cash_amount[0], 0, 1),
         trade_set, curve_store[0], default_weight, groups, stations,
     )
@@ -407,7 +449,7 @@
     tables = [tables[m] for m in range(groups)]
 
     disc = discounts(left, curves)
-    payload = price(column, scaled, route, disc, tables, stations, total_paths)
+    payload = price(column, left, route, disc, tables, stations, total_paths)
     got = lax.all_to_all(payload, ("ccy", "path"), 0, 0, tiled=True)
     expo, sens = collect(pick, got, groups, slots, nodes)
     return expo, sens[None]

time: 55.7 us -> 54.5 us (0.978)
  Pallas kernels: 31.1 us -> 29.9 us
    pallas_call x1, Pallas kernels: 10.7 us -> 9.87 us  [price(): pl.pallas_call(functools.partial(price_kernel, stations, 1.0 / total_path...]
where the time goes in v4:
time: 54.5 us; the launch traced here: 54.4 us
  Pallas kernels  29.9 us (55%)
  blocking collectives  11.9 us (22%)
  waiting for transfers between devices  6.32 us (12%)
  starting transfers between devices  5.52 us (10%)
  between operations  0.71 us (1%)
    pallas_call x2, Pallas kernels, build_table(): pl.pallas_call(table_kernel, out_shape=jax.ShapeDtypeStruct((CFG // LANES...  14.4 us
    all_to_all x1, blocking collectives, local(): got = lax.all_to_all(payload, ('ccy', 'path'), 0, 0, tiled=True)  11.9 us
    pallas_call x1, Pallas kernels, price(): pl.pallas_call(functools.partial(price_kernel, stations, 1.0 / total_path...  9.87 us
    ppermute x6, waiting for transfers between devices, swap(): return lax.ppermute(array, 'ccy', [(i, i ^ mask) for i in range(groups)])  6.32 us
    ppermute x6, starting transfers between devices, swap(): return lax.ppermute(array, 'ccy', [(i, i ^ mask) for i in range(groups)])  5.52 us
    pallas_call x1, Pallas kernels, prepare(): pl.pallas_call(functools.partial(prepare_kernel, groups, stations, 1.0 /...  2.61 us
    pallas_call x1, Pallas kernels, discounts(): pl.pallas_call(functools.partial(disc_kernel, groups), out_shape=jax.Shap...  2.33 us
  transfers between devices with their start and end apart: 6, of which 3 were waited for; matrix products, arithmetic and copies ran while one was open for 0% of the time, Pallas kernels for 31%

profile of v4, /device:TPU:0, one launch (start us, length us, event | category | flops | bytes accessed | tf_op | source)
XLA Modules:
  0.0 54.4 jit_solution(8117448538382755439)
XLA Ops:
  0.6 2.6 %prepare.1 = (f32[32,2048]{1,0:T(8,128)S(1)}, bf16[2,2,1024,128]{3,2,1,0:T(8,128)(2,1)S(1)}, f32[2,512,128]{2,1,0:T(8,128)S(1)}, f32[16,16,128]{2,1,0:T(8,128)S(...) custom-call(s32[16,2048]{1,0:T(8,128)} %bitcast.9, ...), custom_call_target="tpu_custom_call" | custom-call | flops 4194304 | bytes 2097152 | tf_op jit(solution)/shard_map/prepare/pallas_call | solution.py:206
  3.2 3.0 %collective-permute-start.4 = (f32[32,2048]{1,0:T(8,128)S(1)}, f32[32,2048]{1,0:T(8,128)S(1)}, u32[]{:S(2)}, u32[]{:S(2)}) collective-permute-start(f32[32,2048]{1,0:T(8,128)S(1)} %get-tuple-element.21.flow_ref), channel_id=1, source_target_pairs={{0,16},{8,24},{16,0},{24,8},{1,17},{9,25},{17,1},{25,9},{2,18},{10... | collective-permute-start | bytes 786440 | tf_op jit(solution)/shard_map/ppermute | solution.py:435
  6.3 7.1 %shard_map.77.refs_0_ = bf16[8,512,128]{2,1,0:T(8,128)(2,1)S(1)} custom-call(f32[32,2048]{1,0:T(8,128)S(1)} %get-tuple-element.21.flow_ref), custom_call_target="tpu_custom_call" | custom-call | flops 4294967296 | bytes 2097152 | tf_op jit(solution)/shard_map/pallas_call | solution.py:109
  13.4 0.1 collective-permute-start.3
  13.5 0.0 collective-permute-done.4.flow_ref
  13.5 7.3 %shard_map.78.refs_2_ = bf16[8,512,128]{2,1,0:T(8,128)(2,1)S(1)} custom-call(f32[32,2048]{1,0:T(8,128)S(1)} %collective-permute-done.4.flow_ref), custom_call_target="tpu_custom_call" | custom-call | flops 4294967296 | bytes 2097152 | tf_op jit(solution)/shard_map/pallas_call | solution.py:109
  20.8 0.6 %collective-permute-start.5 = (bf16[8,512,128]{2,1,0:T(8,128)(2,1)S(1)}, bf16[8,512,128]{2,1,0:T(8,128)(2,1)S(1)}, u32[]{:S(2)}, u32[]{:S(2)}) collective-permute-start(bf16[8,512,128]{2,1,0:T(8,128)(2,1)S(1)} %shard_map.78.refs_2_), channel_id=1, source_target_pairs={{0,8},{8,0},{16,24},{24,16},{1,9},{9,1},{17,25},{25,17},{2,10},{10... | collective-permute-start | bytes 3145736 | tf_op jit(solution)/shard_map/ppermute | solution.py:435
  21.3 0.1 collective-permute-start
  21.4 0.8 %collective-permute-start.1 = (bf16[2,64,512]{2,1,0:T(8,128)(2,1)S(1)}, bf16[2,64,512]{2,1,0:T(8,128)(2,1)S(1)}, u32[]{:S(2)}, u32[]{:S(2)}) collective-permute-start(bf16[2,64,512]{2,1,0:T(8,128)(2,1)S(1)} %get-tuple-element.19), channel_id=1, source_target_pairs={{0,16},{8,24},{16,0},{24,8},{1,17},{9,25},{17,1},{25,9},{2,18},{10... | collective-permute-start | bytes 393224 | tf_op jit(solution)/shard_map/ppermute | solution.py:435
  22.2 1.0 %collective-permute-start.2 = (bf16[2,64,512]{2,1,0:T(8,128)(2,1)S(1)}, bf16[2,64,512]{2,1,0:T(8,128)(2,1)S(1)}, u32[]{:S(2)}, u32[]{:S(2)}) collective-permute-start(bf16[2,64,512]{2,1,0:T(8,128)(2,1)S(1)} %get-tuple-element.20), channel_id=1, source_target_pairs={{0,24},{8,16},{16,8},{24,0},{1,25},{9,17},{17,9},{25,1},{2,26},{10... | collective-permute-start | bytes 393224 | tf_op jit(solution)/shard_map/ppermute | solution.py:435
  23.2 0.6 %collective-permute-done.refs_1_ = bf16[2,64,512]{2,1,0:T(8,128)(2,1)S(1)} collective-permute-done((bf16[2,64,512]{2,1,0:T(8,128)(2,1)S(1)}, bf16[2,64,512]{2,1,0:T(8,128)(2,1)S(1)}, u32[]{:S(2)}, u32[]{:S(2)}) %collective-permute-start) | collective-permute-done | bytes 131104 | tf_op jit(solution)/shard_map/ppermute | solution.py:435
  23.8 4.0 %collective-permute-done.1.refs_2_ = bf16[2,64,512]{2,1,0:T(8,128)(2,1)S(1)} collective-permute-done((bf16[2,64,512]{2,1,0:T(8,128)(2,1)S(1)}, bf16[2,64,512]{2,1,0:T(8,128)(2,1)S(1)}, u32[]{:S(2)}, u32[]{:S(2)}) %collective-permute-start.1) | collective-permute-done | bytes 131104 | tf_op jit(solution)/shard_map/ppermute | solution.py:435
  27.8 1.7 %collective-permute-done.2.refs_3_ = bf16[2,64,512]{2,1,0:T(8,128)(2,1)S(1)} collective-permute-done((bf16[2,64,512]{2,1,0:T(8,128)(2,1)S(1)}, bf16[2,64,512]{2,1,0:T(8,128)(2,1)S(1)}, u32[]{:S(2)}, u32[]{:S(2)}) %collective-permute-start.2) | collective-permute-done | bytes 131104 | tf_op jit(solution)/shard_map/ppermute | solution.py:435
  29.5 2.3 %discounts.1.disc_ref = bf16[2,4,4,1024,128]{4,3,2,1,0:T(8,128)(2,1)S(1)} custom-call(bf16[2,2,1024,128]{3,2,1,0:T(8,128)(2,1)S(1)} %get-tuple-element.15.left_ref, bf16[2,64,512]{2,1,0:T(8,128)(2,1)S(1)} %get-tuple-element.17.refs_0_, bf16[2,64,512]{2,1,0:T(8,128)(2,1)S(1)} %collective-permute-done.refs_1_, ...), custom_call_target="tpu_custom_call" | custom-call | flops 2147483648 | bytes 8388608 | tf_op jit(solution)/shard_map/discounts/pallas_call | solution.py:251
  31.8 0.0 collective-permute-done.3.refs_1_
  31.8 0.0 collective-permute-done.5.refs_3_
  31.9 9.9 %price.1 = f32[32,1,384]{2,1,0:T(1,128)S(1)} custom-call(f32[2,512,128]{2,1,0:T(8,128)S(1)} %get-tuple-element.14.column_ref, bf16[2,2,1024,128]{3,2,1,0:T(8,128)(2,1)S(1)} %get-tuple-element.15.left_ref, f32[16,8,128]{2,1,0:T(8,128)S(1)} %get-tuple-element.16.route_ref, bf16[2,4,4,1024,128]{4,3,2,1,0:T(8,128)(2,1)S(1)} %discounts.1.disc_ref, ...), custom_call_target="tpu_custom_call" | custom-call | flops 8589934592 | bytes 8388608 | tf_op jit(solution)/shard_map/price/pallas_call | solution.py:369
  41.7 11.9 %all_to_all.5.got_ref = f32[32,1,384]{2,1,0:T(1,128)S(1)} all-to-all(f32[32,1,384]{2,1,0:T(1,128)S(1)} %price.1), channel_id=1, replica_groups=mesh['ccy'=4,'path'=8] {'ccy','path'}, dimensions={0} | all-to-all | bytes 98304 | tf_op jit(solution)/shard_map/all_to_all | solution.py:453
  53.7 0.7 %collect.1 = (f32[16,128]{1,0:T(8,128)}, f32[16,64]{1,0:T(8,128)}) custom-call(f32[16,16,128]{2,1,0:T(8,128)S(1)} %get-tuple-element.13.pick_ref, f32[32,1,384]{2,1,0:T(1,128)S(1)} %all_to_all.5.got_ref), custom_call_target="tpu_custom_call" | custom-call | tf_op jit(solution)/shard_map/collect/pallas_call | solution.py:416
Async XLA Ops:
  3.2 10.2 %collective-permute-start.4 = (f32[32,2048]{1,0:T(8,128)S(1)}, f32[32,2048]{1,0:T(8,128)S(1)}, u32[]{:S(2)}, u32[]{:S(2)}) collective-permute-start(f32[32,2048]{1,0:T(8,128)S(1)} %get-tuple-element.21.flow_ref), channel_id=1, source_target_pairs={{0,16},{8,24},{16,0},{24,8},{1,17},{9,25},{17,1},{25,9},{2,18},{10... | collective-permute-start | bytes 786440 | tf_op jit(solution)/shard_map/ppermute | solution.py:435
  13.4 18.4 %collective-permute-start.3 = (bf16[8,512,128]{2,1,0:T(8,128)(2,1)S(1)}, bf16[8,512,128]{2,1,0:T(8,128)(2,1)S(1)}, u32[]{:S(2)}, u32[]{:S(2)}) collective-permute-start(bf16[8,512,128]{2,1,0:T(8,128)(2,1)S(1)} %shard_map.77.refs_0_), channel_id=1, source_target_pairs={{0,8},{8,0},{16,24},{24,16},{1,9},{9,1},{17,25},{25,17},{2,10},{10... | collective-permute-start | bytes 3145736 | tf_op jit(solution)/shard_map/ppermute | solution.py:435
  20.8 11.1 %collective-permute-start.5 = (bf16[8,512,128]{2,1,0:T(8,128)(2,1)S(1)}, bf16[8,512,128]{2,1,0:T(8,128)(2,1)S(1)}, u32[]{:S(2)}, u32[]{:S(2)}) collective-permute-start(bf16[8,512,128]{2,1,0:T(8,128)(2,1)S(1)} %shard_map.78.refs_2_), channel_id=1, source_target_pairs={{0,8},{8,0},{16,24},{24,16},{1,9},{9,1},{17,25},{25,17},{2,10},{10... | collective-permute-start | bytes 3145736 | tf_op jit(solution)/shard_map/ppermute | solution.py:435
  21.3 2.5 %collective-permute-start = (bf16[2,64,512]{2,1,0:T(8,128)(2,1)S(1)}, bf16[2,64,512]{2,1,0:T(8,128)(2,1)S(1)}, u32[]{:S(2)}, u32[]{:S(2)}) collective-permute-start(bf16[2,64,512]{2,1,0:T(8,128)(2,1)S(1)} %get-tuple-element.18), channel_id=1, source_target_pairs={{0,8},{8,0},{16,24},{24,16},{1,9},{9,1},{17,25},{25,17},{2,10},{10... | collective-permute-start | bytes 393224 | tf_op jit(solution)/shard_map/ppermute | solution.py:435
  21.4 6.4 %collective-permute-start.1 = (bf16[2,64,512]{2,1,0:T(8,128)(2,1)S(1)}, bf16[2,64,512]{2,1,0:T(8,128)(2,1)S(1)}, u32[]{:S(2)}, u32[]{:S(2)}) collective-permute-start(bf16[2,64,512]{2,1,0:T(8,128)(2,1)S(1)} %get-tuple-element.19), channel_id=1, source_target_pairs={{0,16},{8,24},{16,0},{24,8},{1,17},{9,25},{17,1},{25,9},{2,18},{10... | collective-permute-start | bytes 393224 | tf_op jit(solution)/shard_map/ppermute | solution.py:435
  22.2 7.3 %collective-permute-start.2 = (bf16[2,64,512]{2,1,0:T(8,128)(2,1)S(1)}, bf16[2,64,512]{2,1,0:T(8,128)(2,1)S(1)}, u32[]{:S(2)}, u32[]{:S(2)}) collective-permute-start(bf16[2,64,512]{2,1,0:T(8,128)(2,1)S(1)} %get-tuple-element.20), channel_id=1, source_target_pairs={{0,24},{8,16},{16,8},{24,0},{1,25},{9,17},{17,9},{25,1},{2,26},{10... | collective-permute-start | bytes 393224 | tf_op jit(solution)/shard_map/ppermute | solution.py:435

commit v5 on v4

--- a/solution.py
+++ b/solution.py
@@ -38,7 +38,7 @@
     return jnp.concatenate([ref[b] for b in blocks], axis=1)
 
 
-def table_kernel(flow_ref, out_ref, date_t, high_t, one_hot, slot_a, slot_b, acc_ref):
+def table_kernel(flow_ref, out_ref, date_t, high_t, one_hot, slot_a, slot_b):
     ncf, trades = flow_ref.shape[0] // 2, flow_ref.shape[1]
     blocks = trades // LANES
     row_ids = lax.broadcasted_iota(jnp.int32, (NSETS // SUB, SUB, LANES), 0) * SUB
@@ -65,9 +65,10 @@
 
     lax.fori_loop(0, blocks, prepare, 0)
 
-    chunk, tiles = 8, 8
+    tiles = 8
     step = tiles * SUB
     parts = CFG // WIDE
+    chunk = blocks // 2
     base = lax.broadcasted_iota(jnp.int32, (tiles, SUB, LANES), 0) * SUB
     base = base + lax.broadcasted_iota(jnp.int32, (tiles, SUB, LANES), 1)
     slots = (slot_a, slot_b)
@@ -81,26 +82,26 @@
                 acc = jnp.where(want == date_t[b, rows, :][None], high_t[b, rows, :][None], acc)
             slot[b, r : r + step, :] = acc.reshape(step, LANES)
 
-    for part in range(parts + 1):
+    def multiply(slot, part, rows):
+        left = jnp.concatenate([one_hot[b, rows, :] for b in range(blocks)], axis=1)
+        block = dot16(left, join(slot, range(blocks)), NT).astype(jnp.bfloat16)
+        for i in range(WIDE // LANES):
+            place = part * (WIDE // LANES) + i
+            out_ref[place, rows, :] = block[:, i * LANES : (i + 1) * LANES]
+
+    for part in range(parts):
         target, source = slots[part % 2], slots[(part + 1) % 2]
-        if part > 0:
-            acc_ref[...] = jnp.zeros_like(acc_ref)
 
         def body(q, carry, part=part, target=target, source=source):
-            mine = [q * chunk + i for i in range(chunk)]
             if part > 0:
-                acc_ref[...] += dot16(join(one_hot, mine), join(source, mine), NT)
-            if part < parts:
-                for b in mine:
-                    fill(target, part, b)
+                half = pl.ds(pl.multiple_of(q * (NSETS // 2), NSETS // 2), NSETS // 2)
+                multiply(source, part - 1, half)
+            for i in range(chunk):
+                fill(target, part, q * chunk + i)
             return carry
 
-        lax.fori_loop(0, blocks // chunk, body, 0)
-        if part > 0:
-            block = acc_ref[...].astype(jnp.bfloat16)
-            for i in range(WIDE // LANES):
-                place = (part - 1) * (WIDE // LANES) + i
-                out_ref[place] = block[:, i * LANES : (i + 1) * LANES]
+        lax.fori_loop(0, 2, body, 0)
+    multiply(slots[(parts + 1) % 2], parts - 1, slice(0, NSETS))
 
 
 def build_table(flows):
@@ -117,7 +118,6 @@
             pltpu.VMEM((blocks, NSETS, LANES), jnp.bfloat16),
             pltpu.VMEM((blocks, WIDE, LANES), jnp.bfloat16),
             pltpu.VMEM((blocks, WIDE, LANES), jnp.bfloat16),
-            pltpu.VMEM((NSETS, WIDE), jnp.float32),
         ],
         cost_estimate=pl.CostEstimate(
             flops=4 * trades * NSETS * CFG, bytes_accessed=2**21, transcendentals=0
@@ -135,36 +135,22 @@
     ]
     for copy in copies:
         copy.start()
-    for copy in copies:
-        copy.wait()
     index_ref, amount_ref, set_ref, curve_ref, weight_ref, slot_ref = scratch[:6]
     ncf = index_ref.shape[0]
     slots, nodes, total_paths = curve_ref.shape
     paths = total_paths // groups
     dates = slot_ref.shape[0]
     station, member = lax.axis_index("path"), lax.axis_index("ccy")
-    date = index_ref[...]
-    flow_ref[:ncf, :] = (date + CFG * set_ref[...]).astype(jnp.float32)
-    total = jnp.zeros(date.shape, jnp.float32)
-    for k in range(ncf):
-        same = date == index_ref[k : k + 1, :]
-        total = total + jnp.where(same, amount_ref[k : k + 1, :], 0.0)
-    flow_ref[ncf:, :] = total
-    for mask, piece in enumerate(pieces):
-        begin = pl.multiple_of((member ^ mask) * paths, LANES)
-        for k in range(slots):
-            piece[k] = curve_ref[k, :, pl.ds(begin, paths)]
-    lead = (lax.broadcasted_iota(jnp.int32, (8, LANES), 0) == 0).astype(jnp.float32)
-    starts = []
+    copies[5].wait()
+    starts, lines = [], []
     for k in range(slots):
         date, found = 0, 0
         for d in range(dates):
             hit = slot_ref[d] == station * slots + k
             date = jnp.where(hit, d, date)
             found = jnp.where(hit, 1, found)
-        row = weight_ref[pl.ds(date, 1), :] * (0.5 * scale) * found.astype(jnp.float32)
-        column_ref[k] = dot_full(jnp.broadcast_to(row, (8, NSETS)), lead, TN)
         starts.append(0.5 * (date.astype(jnp.float32) + 1.0))
+        lines.append((date, found))
     lane = lax.broadcasted_iota(jnp.int32, (CFG, slots * nodes), 1)
     start = jnp.zeros((CFG, slots * nodes), jnp.float32)
     for k in range(slots):
@@ -196,6 +182,37 @@
         for m in range(groups):
             chosen = ((member ^ g) == m).astype(jnp.float32)
             route_ref[g * groups + m] = jnp.full((8, LANES), chosen, jnp.float32)
+    for copy in copies[:5]:
+        copy.wait()
+
+    def pack(b, carry):
+        cols = pl.ds(pl.multiple_of(b * LANES, LANES), LANES)
+        date, amount = index_ref[:, cols], amount_ref[:, cols]
+        flow_ref[:ncf, cols] = (date + CFG * set_ref[:, cols]).astype(jnp.float32)
+        total = jnp.zeros((ncf, LANES), jnp.float32)
+        for k in range(ncf):
+            same = date == date[k : k + 1, :]
+            total = total + jnp.where(same, amount[k : k + 1, :], 0.0)
+        flow_ref[ncf:, cols] = total
+        return carry
+
+    lax.fori_loop(0, index_ref.shape[1] // LANES, pack, 0)
+    for mask, piece in enumerate(pieces):
+        begin = pl.multiple_of((member ^ mask) * paths, LANES)
+        for k in range(slots):
+            piece[k] = curve_ref[k, :, pl.ds(begin, paths)]
+    term = lax.broadcasted_iota(jnp.int32, (SUB, NSETS), 0)
+    for k, (date, found) in enumerate(lines):
+        row = weight_ref[pl.ds(date, 1), :] * (0.5 * scale) * found.astype(jnp.float32)
+        rest = jnp.broadcast_to(row, (SUB, NSETS))
+        terms = jnp.zeros((SUB, NSETS), jnp.float32)
+        for i in range(3):
+            part = rest.astype(jnp.bfloat16).astype(jnp.float32)
+            terms = jnp.where(term == i, part, terms)
+            rest = rest - part
+        column_ref[k] = dot16(
+            terms.astype(jnp.bfloat16), jnp.ones((SUB, LANES), jnp.bfloat16), TN
+        )
 
 
 def prepare(date_slot, index, amount, sets, curve, weights, groups, stations):

time: 54.5 us -> 53.3 us (0.978)
  Pallas kernels: 29.9 us -> 28.1 us
    pallas_call x2, Pallas kernels: 14.4 us -> 13.1 us  [build_table(): pl.pallas_call(table_kernel, out_shape=jax.ShapeDtypeStruct((CFG // LANES...]
  transfers between devices with their start and end apart: 6 -> 6, of which waited for: 3 -> 3; matrix products, arithmetic and copies ran while one was open for 0% -> 0% of each run, Pallas kernels for 31% -> 29%
where the time goes in v5:
time: 53.3 us; the launch traced here: 53.1 us
  Pallas kernels  28.1 us (53%)
  blocking collectives  12.4 us (23%)
  waiting for transfers between devices  6.32 us (12%)
  starting transfers between devices  5.51 us (10%)
  between operations  0.71 us (1%)
    pallas_call x2, Pallas kernels, build_table(): pl.pallas_call(table_kernel, out_shape=jax.ShapeDtypeStruct((CFG // LANES...  13.1 us
    all_to_all x1, blocking collectives, local(): got = lax.all_to_all(payload, ('ccy', 'path'), 0, 0, tiled=True)  12.4 us
    pallas_call x1, Pallas kernels, price(): pl.pallas_call(functools.partial(price_kernel, stations, 1.0 / total_path...  9.87 us
    ppermute x6, waiting for transfers between devices, swap(): return lax.ppermute(array, 'ccy', [(i, i ^ mask) for i in range(groups)])  6.32 us
    ppermute x6, starting transfers between devices, swap(): return lax.ppermute(array, 'ccy', [(i, i ^ mask) for i in range(groups)])  5.51 us
    pallas_call x1, Pallas kernels, discounts(): pl.pallas_call(functools.partial(disc_kernel, groups), out_shape=jax.Shap...  2.32 us
    pallas_call x1, Pallas kernels, prepare(): pl.pallas_call(functools.partial(prepare_kernel, groups, stations, 1.0 /...  2.12 us
  transfers between devices with their start and end apart: 6, of which 3 were waited for; matrix products, arithmetic and copies ran while one was open for 0% of the time, Pallas kernels for 29%

profile of v5, /device:TPU:0, one launch (start us, length us, event | category | flops | bytes accessed | tf_op | source)
XLA Modules:
  0.0 53.1 jit_solution(638528992388881085)
XLA Ops:
  0.6 2.1 %prepare.1 = (f32[32,2048]{1,0:T(8,128)S(1)}, bf16[2,2,1024,128]{3,2,1,0:T(8,128)(2,1)S(1)}, f32[2,512,128]{2,1,0:T(8,128)S(1)}, f32[16,16,128]{2,1,0:T(8,128)S(...) custom-call(s32[16,2048]{1,0:T(8,128)} %bitcast.9, ...), custom_call_target="tpu_custom_call" | custom-call | flops 4194304 | bytes 2097152 | tf_op jit(solution)/shard_map/prepare/pallas_call | solution.py:223
  2.8 3.0 %collective-permute-start.4 = (f32[32,2048]{1,0:T(8,128)S(1)}, f32[32,2048]{1,0:T(8,128)S(1)}, u32[]{:S(2)}, u32[]{:S(2)}) collective-permute-start(f32[32,2048]{1,0:T(8,128)S(1)} %get-tuple-element.21.flow_ref), channel_id=1, source_target_pairs={{0,16},{8,24},{16,0},{24,8},{1,17},{9,25},{17,1},{25,9},{2,18},{10... | collective-permute-start | bytes 786440 | tf_op jit(solution)/shard_map/ppermute | solution.py:452
  5.8 6.5 %shard_map.77.refs_0_ = bf16[8,512,128]{2,1,0:T(8,128)(2,1)S(1)} custom-call(f32[32,2048]{1,0:T(8,128)S(1)} %get-tuple-element.21.flow_ref), custom_call_target="tpu_custom_call" | custom-call | flops 4294967296 | bytes 2097152 | tf_op jit(solution)/shard_map/pallas_call | solution.py:110
  12.3 0.1 collective-permute-start.3
  12.4 0.0 collective-permute-done.4.flow_ref
  12.4 6.7 %shard_map.78.refs_2_ = bf16[8,512,128]{2,1,0:T(8,128)(2,1)S(1)} custom-call(f32[32,2048]{1,0:T(8,128)S(1)} %collective-permute-done.4.flow_ref), custom_call_target="tpu_custom_call" | custom-call | flops 4294967296 | bytes 2097152 | tf_op jit(solution)/shard_map/pallas_call | solution.py:110
  19.0 0.6 %collective-permute-start.5 = (bf16[8,512,128]{2,1,0:T(8,128)(2,1)S(1)}, bf16[8,512,128]{2,1,0:T(8,128)(2,1)S(1)}, u32[]{:S(2)}, u32[]{:S(2)}) collective-permute-start(bf16[8,512,128]{2,1,0:T(8,128)(2,1)S(1)} %shard_map.78.refs_2_), channel_id=1, source_target_pairs={{0,8},{8,0},{16,24},{24,16},{1,9},{9,1},{17,25},{25,17},{2,10},{10... | collective-permute-start | bytes 3145736 | tf_op jit(solution)/shard_map/ppermute | solution.py:452
  19.6 0.1 collective-permute-start
  19.7 1.4 %collective-permute-start.1 = (bf16[2,64,512]{2,1,0:T(8,128)(2,1)S(1)}, bf16[2,64,512]{2,1,0:T(8,128)(2,1)S(1)}, u32[]{:S(2)}, u32[]{:S(2)}) collective-permute-start(bf16[2,64,512]{2,1,0:T(8,128)(2,1)S(1)} %get-tuple-element.19), channel_id=1, source_target_pairs={{0,16},{8,24},{16,0},{24,8},{1,17},{9,25},{17,1},{25,9},{2,18},{10... | collective-permute-start | bytes 393224 | tf_op jit(solution)/shard_map/ppermute | solution.py:452
  21.1 0.4 collective-permute-start.2
  21.4 0.6 %collective-permute-done.refs_1_ = bf16[2,64,512]{2,1,0:T(8,128)(2,1)S(1)} collective-permute-done((bf16[2,64,512]{2,1,0:T(8,128)(2,1)S(1)}, bf16[2,64,512]{2,1,0:T(8,128)(2,1)S(1)}, u32[]{:S(2)}, u32[]{:S(2)}) %collective-permute-start) | collective-permute-done | bytes 131104 | tf_op jit(solution)/shard_map/ppermute | solution.py:452
  22.1 4.0 %collective-permute-done.1.refs_2_ = bf16[2,64,512]{2,1,0:T(8,128)(2,1)S(1)} collective-permute-done((bf16[2,64,512]{2,1,0:T(8,128)(2,1)S(1)}, bf16[2,64,512]{2,1,0:T(8,128)(2,1)S(1)}, u32[]{:S(2)}, u32[]{:S(2)}) %collective-permute-start.1) | collective-permute-done | bytes 131104 | tf_op jit(solution)/shard_map/ppermute | solution.py:452
  26.0 1.7 %collective-permute-done.2.refs_3_ = bf16[2,64,512]{2,1,0:T(8,128)(2,1)S(1)} collective-permute-done((bf16[2,64,512]{2,1,0:T(8,128)(2,1)S(1)}, bf16[2,64,512]{2,1,0:T(8,128)(2,1)S(1)}, u32[]{:S(2)}, u32[]{:S(2)}) %collective-permute-start.2) | collective-permute-done | bytes 131104 | tf_op jit(solution)/shard_map/ppermute | solution.py:452
  27.8 2.3 %discounts.1.disc_ref = bf16[2,4,4,1024,128]{4,3,2,1,0:T(8,128)(2,1)S(1)} custom-call(bf16[2,2,1024,128]{3,2,1,0:T(8,128)(2,1)S(1)} %get-tuple-element.15.left_ref, bf16[2,64,512]{2,1,0:T(8,128)(2,1)S(1)} %get-tuple-element.17.refs_0_, bf16[2,64,512]{2,1,0:T(8,128)(2,1)S(1)} %collective-permute-done.refs_1_, ...), custom_call_target="tpu_custom_call" | custom-call | flops 2147483648 | bytes 8388608 | tf_op jit(solution)/shard_map/discounts/pallas_call | solution.py:268
  30.1 0.0 collective-permute-done.3.refs_1_
  30.1 0.0 collective-permute-done.5.refs_3_
  30.1 9.9 %price.1 = f32[32,1,384]{2,1,0:T(1,128)S(1)} custom-call(f32[2,512,128]{2,1,0:T(8,128)S(1)} %get-tuple-element.14.column_ref, bf16[2,2,1024,128]{3,2,1,0:T(8,128)(2,1)S(1)} %get-tuple-element.15.left_ref, f32[16,8,128]{2,1,0:T(8,128)S(1)} %get-tuple-element.16.route_ref, bf16[2,4,4,1024,128]{4,3,2,1,0:T(8,128)(2,1)S(1)} %discounts.1.disc_ref, ...), custom_call_target="tpu_custom_call" | custom-call | flops 8589934592 | bytes 8388608 | tf_op jit(solution)/shard_map/price/pallas_call | solution.py:386
  40.0 12.4 %all_to_all.5.got_ref = f32[32,1,384]{2,1,0:T(1,128)S(1)} all-to-all(f32[32,1,384]{2,1,0:T(1,128)S(1)} %price.1), channel_id=1, replica_groups=mesh['ccy'=4,'path'=8] {'ccy','path'}, dimensions={0} | all-to-all | bytes 98304 | tf_op jit(solution)/shard_map/all_to_all | solution.py:470
  52.4 0.7 %collect.1 = (f32[16,128]{1,0:T(8,128)}, f32[16,64]{1,0:T(8,128)}) custom-call(f32[16,16,128]{2,1,0:T(8,128)S(1)} %get-tuple-element.13.pick_ref, f32[32,1,384]{2,1,0:T(1,128)S(1)} %all_to_all.5.got_ref), custom_call_target="tpu_custom_call" | custom-call | tf_op jit(solution)/shard_map/collect/pallas_call | solution.py:433
Async XLA Ops:
  2.8 9.6 %collective-permute-start.4 = (f32[32,2048]{1,0:T(8,128)S(1)}, f32[32,2048]{1,0:T(8,128)S(1)}, u32[]{:S(2)}, u32[]{:S(2)}) collective-permute-start(f32[32,2048]{1,0:T(8,128)S(1)} %get-tuple-element.21.flow_ref), channel_id=1, source_target_pairs={{0,16},{8,24},{16,0},{24,8},{1,17},{9,25},{17,1},{25,9},{2,18},{10... | collective-permute-start | bytes 786440 | tf_op jit(solution)/shard_map/ppermute | solution.py:452
  12.3 17.8 %collective-permute-start.3 = (bf16[8,512,128]{2,1,0:T(8,128)(2,1)S(1)}, bf16[8,512,128]{2,1,0:T(8,128)(2,1)S(1)}, u32[]{:S(2)}, u32[]{:S(2)}) collective-permute-start(bf16[8,512,128]{2,1,0:T(8,128)(2,1)S(1)} %shard_map.77.refs_0_), channel_id=1, source_target_pairs={{0,8},{8,0},{16,24},{24,16},{1,9},{9,1},{17,25},{25,17},{2,10},{10... | collective-permute-start | bytes 3145736 | tf_op jit(solution)/shard_map/ppermute | solution.py:452
  19.0 11.1 %collective-permute-start.5 = (bf16[8,512,128]{2,1,0:T(8,128)(2,1)S(1)}, bf16[8,512,128]{2,1,0:T(8,128)(2,1)S(1)}, u32[]{:S(2)}, u32[]{:S(2)}) collective-permute-start(bf16[8,512,128]{2,1,0:T(8,128)(2,1)S(1)} %shard_map.78.refs_2_), channel_id=1, source_target_pairs={{0,8},{8,0},{16,24},{24,16},{1,9},{9,1},{17,25},{25,17},{2,10},{10... | collective-permute-start | bytes 3145736 | tf_op jit(solution)/shard_map/ppermute | solution.py:452
  19.6 2.5 %collective-permute-start = (bf16[2,64,512]{2,1,0:T(8,128)(2,1)S(1)}, bf16[2,64,512]{2,1,0:T(8,128)(2,1)S(1)}, u32[]{:S(2)}, u32[]{:S(2)}) collective-permute-start(bf16[2,64,512]{2,1,0:T(8,128)(2,1)S(1)} %get-tuple-element.18), channel_id=1, source_target_pairs={{0,8},{8,0},{16,24},{24,16},{1,9},{9,1},{17,25},{25,17},{2,10},{10... | collective-permute-start | bytes 393224 | tf_op jit(solution)/shard_map/ppermute | solution.py:452
  19.7 6.4 %collective-permute-start.1 = (bf16[2,64,512]{2,1,0:T(8,128)(2,1)S(1)}, bf16[2,64,512]{2,1,0:T(8,128)(2,1)S(1)}, u32[]{:S(2)}, u32[]{:S(2)}) collective-permute-start(bf16[2,64,512]{2,1,0:T(8,128)(2,1)S(1)} %get-tuple-element.19), channel_id=1, source_target_pairs={{0,16},{8,24},{16,0},{24,8},{1,17},{9,25},{17,1},{25,9},{2,18},{10... | collective-permute-start | bytes 393224 | tf_op jit(solution)/shard_map/ppermute | solution.py:452
  21.1 6.7 %collective-permute-start.2 = (bf16[2,64,512]{2,1,0:T(8,128)(2,1)S(1)}, bf16[2,64,512]{2,1,0:T(8,128)(2,1)S(1)}, u32[]{:S(2)}, u32[]{:S(2)}) collective-permute-start(bf16[2,64,512]{2,1,0:T(8,128)(2,1)S(1)} %get-tuple-element.20), channel_id=1, source_target_pairs={{0,24},{8,16},{16,8},{24,0},{1,25},{9,17},{17,9},{25,1},{2,26},{10... | collective-permute-start | bytes 393224 | tf_op jit(solution)/shard_map/ppermute | solution.py:452

commit v6 on v5

--- a/solution.py
+++ b/solution.py
@@ -26,12 +26,6 @@
 
 def dot16(a, b, dims):
     return lax.dot_general(a, b, dims, preferred_element_type=jnp.float32)
-
-
-def dot_full(a, b, dims):
-    return lax.dot_general(
-        a, b, dims, precision=lax.Precision.HIGHEST, preferred_element_type=jnp.float32
-    )
 
 
 def join(ref, blocks):
@@ -65,7 +59,7 @@
 
     lax.fori_loop(0, blocks, prepare, 0)
 
-    tiles = 8
+    tiles = 16
     step = tiles * SUB
     parts = CFG // WIDE
     chunk = blocks // 2
@@ -316,7 +310,11 @@
             folded = folded + (part + square * inverse)
             slope = column + column * (part * inverse)
             slope_ref[k, p] = slope.astype(jnp.bfloat16)
-        summed = dot_full(jnp.ones((8, LANES), jnp.float32), folded, NT)
+        summed = jnp.zeros((SUB, NSETS), jnp.float32)
+        for _ in range(3):
+            term = folded.astype(jnp.bfloat16)
+            folded = folded - term.astype(jnp.float32)
+            summed = summed + dot16(jnp.ones((SUB, LANES), jnp.bfloat16), term, NT)
         expo_ref[k : k + 1, :] = summed[0:1] * (0.5 * scale)
 
     def pulls(k, g):

time: 53.3 us -> 53.2 us (level)
  no operation moved by 1% of the time
where the time goes in v6:
time: 53.2 us; the launch traced here: 53 us
  Pallas kernels  28 us (53%)
  blocking collectives  12.5 us (23%)
  waiting for transfers between devices  6.32 us (12%)
  starting transfers between devices  5.51 us (10%)
  between operations  0.71 us (1%)
    pallas_call x2, Pallas kernels, build_table(): pl.pallas_call(table_kernel, out_shape=jax.ShapeDtypeStruct((CFG // LANES...  13 us
    all_to_all x1, blocking collectives, local(): got = lax.all_to_all(payload, ('ccy', 'path'), 0, 0, tiled=True)  12.5 us
    pallas_call x1, Pallas kernels, price(): pl.pallas_call(functools.partial(price_kernel, stations, 1.0 / total_path...  9.8 us
    ppermute x6, waiting for transfers between devices, swap(): return lax.ppermute(array, 'ccy', [(i, i ^ mask) for i in range(groups)])  6.32 us
    ppermute x6, starting transfers between devices, swap(): return lax.ppermute(array, 'ccy', [(i, i ^ mask) for i in range(groups)])  5.51 us
    pallas_call x1, Pallas kernels, discounts(): pl.pallas_call(functools.partial(disc_kernel, groups), out_shape=jax.Shap...  2.32 us
    pallas_call x1, Pallas kernels, prepare(): pl.pallas_call(functools.partial(prepare_kernel, groups, stations, 1.0 /...  2.12 us
  transfers between devices with their start and end apart: 6, of which 3 were waited for; matrix products, arithmetic and copies ran while one was open for 0% of the time, Pallas kernels for 29%

profile of v6, /device:TPU:0, one launch (start us, length us, event | category | flops | bytes accessed | tf_op | source)
XLA Modules:
  0.0 53.0 jit_solution(4972318938687058547)
XLA Ops:
  0.6 2.1 %prepare.1 = (f32[32,2048]{1,0:T(8,128)S(1)}, bf16[2,2,1024,128]{3,2,1,0:T(8,128)(2,1)S(1)}, f32[2,512,128]{2,1,0:T(8,128)S(1)}, f32[16,16,128]{2,1,0:T(8,128)S(...) custom-call(s32[16,2048]{1,0:T(8,128)} %bitcast.9, ...), custom_call_target="tpu_custom_call" | custom-call | flops 4194304 | bytes 2097152 | tf_op jit(solution)/shard_map/prepare/pallas_call | solution.py:217
  2.8 3.0 %collective-permute-start.4 = (f32[32,2048]{1,0:T(8,128)S(1)}, f32[32,2048]{1,0:T(8,128)S(1)}, u32[]{:S(2)}, u32[]{:S(2)}) collective-permute-start(f32[32,2048]{1,0:T(8,128)S(1)} %get-tuple-element.21.flow_ref), channel_id=1, source_target_pairs={{0,16},{8,24},{16,0},{24,8},{1,17},{9,25},{17,1},{25,9},{2,18},{10... | collective-permute-start | bytes 786440 | tf_op jit(solution)/shard_map/ppermute | solution.py:450
  5.8 6.4 %shard_map.77.refs_0_ = bf16[8,512,128]{2,1,0:T(8,128)(2,1)S(1)} custom-call(f32[32,2048]{1,0:T(8,128)S(1)} %get-tuple-element.21.flow_ref), custom_call_target="tpu_custom_call" | custom-call | flops 4294967296 | bytes 2097152 | tf_op jit(solution)/shard_map/pallas_call | solution.py:104
  12.2 0.1 collective-permute-start.3
  12.3 0.0 collective-permute-done.4.flow_ref
  12.3 6.6 %shard_map.78.refs_2_ = bf16[8,512,128]{2,1,0:T(8,128)(2,1)S(1)} custom-call(f32[32,2048]{1,0:T(8,128)S(1)} %collective-permute-done.4.flow_ref), custom_call_target="tpu_custom_call" | custom-call | flops 4294967296 | bytes 2097152 | tf_op jit(solution)/shard_map/pallas_call | solution.py:104
  18.9 0.6 %collective-permute-start.5 = (bf16[8,512,128]{2,1,0:T(8,128)(2,1)S(1)}, bf16[8,512,128]{2,1,0:T(8,128)(2,1)S(1)}, u32[]{:S(2)}, u32[]{:S(2)}) collective-permute-start(bf16[8,512,128]{2,1,0:T(8,128)(2,1)S(1)} %shard_map.78.refs_2_), channel_id=1, source_target_pairs={{0,8},{8,0},{16,24},{24,16},{1,9},{9,1},{17,25},{25,17},{2,10},{10... | collective-permute-start | bytes 3145736 | tf_op jit(solution)/shard_map/ppermute | solution.py:450
  19.5 0.1 collective-permute-start
  19.6 1.5 %collective-permute-start.1 = (bf16[2,64,512]{2,1,0:T(8,128)(2,1)S(1)}, bf16[2,64,512]{2,1,0:T(8,128)(2,1)S(1)}, u32[]{:S(2)}, u32[]{:S(2)}) collective-permute-start(bf16[2,64,512]{2,1,0:T(8,128)(2,1)S(1)} %get-tuple-element.19), channel_id=1, source_target_pairs={{0,16},{8,24},{16,0},{24,8},{1,17},{9,25},{17,1},{25,9},{2,18},{10... | collective-permute-start | bytes 393224 | tf_op jit(solution)/shard_map/ppermute | solution.py:450
  21.0 0.3 collective-permute-start.2
  21.4 0.6 %collective-permute-done.refs_1_ = bf16[2,64,512]{2,1,0:T(8,128)(2,1)S(1)} collective-permute-done((bf16[2,64,512]{2,1,0:T(8,128)(2,1)S(1)}, bf16[2,64,512]{2,1,0:T(8,128)(2,1)S(1)}, u32[]{:S(2)}, u32[]{:S(2)}) %collective-permute-start) | collective-permute-done | bytes 131104 | tf_op jit(solution)/shard_map/ppermute | solution.py:450
  22.0 4.0 %collective-permute-done.1.refs_2_ = bf16[2,64,512]{2,1,0:T(8,128)(2,1)S(1)} collective-permute-done((bf16[2,64,512]{2,1,0:T(8,128)(2,1)S(1)}, bf16[2,64,512]{2,1,0:T(8,128)(2,1)S(1)}, u32[]{:S(2)}, u32[]{:S(2)}) %collective-permute-start.1) | collective-permute-done | bytes 131104 | tf_op jit(solution)/shard_map/ppermute | solution.py:450
  25.9 1.7 %collective-permute-done.2.refs_3_ = bf16[2,64,512]{2,1,0:T(8,128)(2,1)S(1)} collective-permute-done((bf16[2,64,512]{2,1,0:T(8,128)(2,1)S(1)}, bf16[2,64,512]{2,1,0:T(8,128)(2,1)S(1)}, u32[]{:S(2)}, u32[]{:S(2)}) %collective-permute-start.2) | collective-permute-done | bytes 131104 | tf_op jit(solution)/shard_map/ppermute | solution.py:450
  27.7 2.3 %discounts.1.disc_ref = bf16[2,4,4,1024,128]{4,3,2,1,0:T(8,128)(2,1)S(1)} custom-call(bf16[2,2,1024,128]{3,2,1,0:T(8,128)(2,1)S(1)} %get-tuple-element.15.left_ref, bf16[2,64,512]{2,1,0:T(8,128)(2,1)S(1)} %get-tuple-element.17.refs_0_, bf16[2,64,512]{2,1,0:T(8,128)(2,1)S(1)} %collective-permute-done.refs_1_, ...), custom_call_target="tpu_custom_call" | custom-call | flops 2147483648 | bytes 8388608 | tf_op jit(solution)/shard_map/discounts/pallas_call | solution.py:262
  30.0 0.0 collective-permute-done.3.refs_1_
  30.0 0.0 collective-permute-done.5.refs_3_
  30.0 9.8 %price.1 = f32[32,1,384]{2,1,0:T(1,128)S(1)} custom-call(f32[2,512,128]{2,1,0:T(8,128)S(1)} %get-tuple-element.14.column_ref, bf16[2,2,1024,128]{3,2,1,0:T(8,128)(2,1)S(1)} %get-tuple-element.15.left_ref, f32[16,8,128]{2,1,0:T(8,128)S(1)} %get-tuple-element.16.route_ref, bf16[2,4,4,1024,128]{4,3,2,1,0:T(8,128)(2,1)S(1)} %discounts.1.disc_ref, ...), custom_call_target="tpu_custom_call" | custom-call | flops 8589934592 | bytes 8388608 | tf_op jit(solution)/shard_map/price/pallas_call | solution.py:384
  39.8 12.5 %all_to_all.5.got_ref = f32[32,1,384]{2,1,0:T(1,128)S(1)} all-to-all(f32[32,1,384]{2,1,0:T(1,128)S(1)} %price.1), channel_id=1, replica_groups=mesh['ccy'=4,'path'=8] {'ccy','path'}, dimensions={0} | all-to-all | bytes 98304 | tf_op jit(solution)/shard_map/all_to_all | solution.py:468
  52.3 0.7 %collect.1 = (f32[16,128]{1,0:T(8,128)}, f32[16,64]{1,0:T(8,128)}) custom-call(f32[16,16,128]{2,1,0:T(8,128)S(1)} %get-tuple-element.13.pick_ref, f32[32,1,384]{2,1,0:T(1,128)S(1)} %all_to_all.5.got_ref), custom_call_target="tpu_custom_call" | custom-call | tf_op jit(solution)/shard_map/collect/pallas_call | solution.py:431
Async XLA Ops:
  2.8 9.6 %collective-permute-start.4 = (f32[32,2048]{1,0:T(8,128)S(1)}, f32[32,2048]{1,0:T(8,128)S(1)}, u32[]{:S(2)}, u32[]{:S(2)}) collective-permute-start(f32[32,2048]{1,0:T(8,128)S(1)} %get-tuple-element.21.flow_ref), channel_id=1, source_target_pairs={{0,16},{8,24},{16,0},{24,8},{1,17},{9,25},{17,1},{25,9},{2,18},{10... | collective-permute-start | bytes 786440 | tf_op jit(solution)/shard_map/ppermute | solution.py:450
  12.2 17.8 %collective-permute-start.3 = (bf16[8,512,128]{2,1,0:T(8,128)(2,1)S(1)}, bf16[8,512,128]{2,1,0:T(8,128)(2,1)S(1)}, u32[]{:S(2)}, u32[]{:S(2)}) collective-permute-start(bf16[8,512,128]{2,1,0:T(8,128)(2,1)S(1)} %shard_map.77.refs_0_), channel_id=1, source_target_pairs={{0,8},{8,0},{16,24},{24,16},{1,9},{9,1},{17,25},{25,17},{2,10},{10... | collective-permute-start | bytes 3145736 | tf_op jit(solution)/shard_map/ppermute | solution.py:450
  18.9 11.1 %collective-permute-start.5 = (bf16[8,512,128]{2,1,0:T(8,128)(2,1)S(1)}, bf16[8,512,128]{2,1,0:T(8,128)(2,1)S(1)}, u32[]{:S(2)}, u32[]{:S(2)}) collective-permute-start(bf16[8,512,128]{2,1,0:T(8,128)(2,1)S(1)} %shard_map.78.refs_2_), channel_id=1, source_target_pairs={{0,8},{8,0},{16,24},{24,16},{1,9},{9,1},{17,25},{25,17},{2,10},{10... | collective-permute-start | bytes 3145736 | tf_op jit(solution)/shard_map/ppermute | solution.py:450
  19.5 2.5 %collective-permute-start = (bf16[2,64,512]{2,1,0:T(8,128)(2,1)S(1)}, bf16[2,64,512]{2,1,0:T(8,128)(2,1)S(1)}, u32[]{:S(2)}, u32[]{:S(2)}) collective-permute-start(bf16[2,64,512]{2,1,0:T(8,128)(2,1)S(1)} %get-tuple-element.18), channel_id=1, source_target_pairs={{0,8},{8,0},{16,24},{24,16},{1,9},{9,1},{17,25},{25,17},{2,10},{10... | collective-permute-start | bytes 393224 | tf_op jit(solution)/shard_map/ppermute | solution.py:450
  19.6 6.4 %collective-permute-start.1 = (bf16[2,64,512]{2,1,0:T(8,128)(2,1)S(1)}, bf16[2,64,512]{2,1,0:T(8,128)(2,1)S(1)}, u32[]{:S(2)}, u32[]{:S(2)}) collective-permute-start(bf16[2,64,512]{2,1,0:T(8,128)(2,1)S(1)} %get-tuple-element.19), channel_id=1, source_target_pairs={{0,16},{8,24},{16,0},{24,8},{1,17},{9,25},{17,1},{25,9},{2,18},{10... | collective-permute-start | bytes 393224 | tf_op jit(solution)/shard_map/ppermute | solution.py:450
  21.0 6.6 %collective-permute-start.2 = (bf16[2,64,512]{2,1,0:T(8,128)(2,1)S(1)}, bf16[2,64,512]{2,1,0:T(8,128)(2,1)S(1)}, u32[]{:S(2)}, u32[]{:S(2)}) collective-permute-start(bf16[2,64,512]{2,1,0:T(8,128)(2,1)S(1)} %get-tuple-element.20), channel_id=1, source_target_pairs={{0,24},{8,16},{16,8},{24,0},{1,25},{9,17},{17,9},{25,1},{2,26},{10... | collective-permute-start | bytes 393224 | tf_op jit(solution)/shard_map/ppermute | solution.py:450
